TPU v7x, 32 devices: a whole 2x2x4 slice. The times are simulated.
32 devices in a mesh: case: 4 (over z), gx: 2 (over y), gy: 4 (over x, core).
Axes of the slice: x: 2, y: 2, z: 4, core: 2. Of those that a mesh axis runs over, the one named last changes fastest.
Arguments:
- load: float32 [8, 24, 32, 128], P(('case', 'gx'), 'gy'), parts along dimension 0, may hold values from -4 to 4
- factors: bfloat16 [4, 8, 24, 128, 128], P(None, ('case', 'gx'), 'gy'), parts along dimension 1, may hold values from -6 to 6
- links: int32 [4, 8, 24], P(None, ('case', 'gx'), 'gy'), parts along dimension 1, may hold values from 0 to 1
- shift: float32 [8, 24, 128], P(('case', 'gx'), 'gy'), parts along dimension 0, may hold values from 0.25 to 2.5
Outputs:
- solution: float32 [8, 24, 32, 128], P(('case', 'gx'), 'gy'), parts along dimension 0
- residual: float32 [8, 24, 32, 128], P(('case', 'gx'), 'gy'), parts along dimension 0
There are 4 independent parts, one for each index of `case`. A program takes and returns all parts, laid end to end along the dimension named above; each array names one. Nothing has to cross between parts.
All inputs are finite; a program needn't handle non-finite values.
Results may differ from a plain program's by a relative error of at most 0.008.
Values may be sent and summed in bfloat16 or wider, within the bound.
No kernel may reach another device: no remote copies, remote signals or barrier semaphores. Data moves between devices by JAX's collectives and lax.ppermute only.
A program may use at most 64 MiB of HBM per device.

v0:
```python
import jax
import jax.numpy as jnp
from jax import lax
from jax.sharding import PartitionSpec as P

B = 128
ITERS = 8


OFFSETS = ((1, 0), (0, 1), (1, 1), (1, -1))
PRECISE = lax.Precision.HIGHEST


def extended(cells, sides, width):
    for axis, dim in sides:
        count = lax.axis_size(axis)
        ends = count - 1
        head = lax.slice_in_dim(cells, 0, width, axis=dim)
        tail = lax.slice_in_dim(cells, cells.shape[dim] - width, cells.shape[dim], axis=dim)
        cells = jnp.concatenate(
            [
                lax.ppermute(tail, axis, [(i, (i + 1) % count) for i in range(ends)]),
                cells,
                lax.ppermute(head, axis, [((i + 1) % count, i) for i in range(ends)]),
            ],
            axis=dim,
        )
    return cells


def window(padded, step_x, step_y, count_x, count_y):
    return padded[1 + step_x : 1 + step_x + count_x, 1 + step_y : 1 + step_y + count_y]


def inner(left, right):
    return jnp.sum(left * right, axis=(0, 1, 3))


def spread(values):
    return values[None, None, :, None]


def local(load, factors, links, shift):
    count_x, count_y = (load.shape[0], load.shape[1])
    masked = factors * links.astype(jnp.bfloat16)[:, :, :, None, None]
    springs = (
        jnp.einsum("dxyak,dxybk->dxyab", masked, masked, preferred_element_type=jnp.float32) / B
    )
    padded_springs = extended(springs, (("gx", 1), ("gy", 2)), 1)
    forward = padded_springs[:, 1:-1, 1:-1]
    backward = jnp.stack(
        [
            window(
                padded_springs[offset], -OFFSETS[offset][0], -OFFSETS[offset][1], count_x, count_y
            )
            for offset in range(4)
        ]
    )
    identity = jnp.eye(B, dtype=jnp.float32)
    diagonal = shift[..., None] * identity + jnp.sum(forward, axis=0) + jnp.sum(backward, axis=0)
    lower = jnp.linalg.cholesky(diagonal.reshape(-1, B, B))
    inverse = jax.vmap(lambda factor: jax.scipy.linalg.cho_solve((factor, True), identity))(
        lower
    ).reshape(diagonal.shape)
    blocks = jnp.concatenate([diagonal[None], -forward, -backward], axis=0)

    def operate(field):
        padded = extended(field, (("gx", 0), ("gy", 1)), 1)
        pieces = [field]
        pieces = pieces + [
            window(padded, step_x, step_y, count_x, count_y) for step_x, step_y in OFFSETS
        ]
        pieces = pieces + [
            window(padded, -step_x, -step_y, count_x, count_y) for step_x, step_y in OFFSETS
        ]
        return jnp.einsum(
            "kxyab,kxyrb->xyra",
            blocks,
            jnp.stack(pieces),
            precision=PRECISE,
            preferred_element_type=jnp.float32,
        )

    def precondition(field):
        return jnp.einsum(
            "xyab,xyrb->xyra", inverse, field, precision=PRECISE, preferred_element_type=jnp.float32
        )

    def paired(residual, precon, image):
        return lax.psum((inner(residual, precon), inner(image, precon)), ("gx", "gy"))

    solution = jnp.zeros_like(load)
    residual = load
    precon = precondition(residual)
    image = operate(precon)
    gamma, delta = paired(residual, precon, image)
    alpha = gamma / delta
    direction, along = (precon, image)
    for iteration in range(ITERS):
        solution = solution + spread(alpha) * direction
        residual = residual - spread(alpha) * along
        if iteration + 1 < ITERS:
            precon = precondition(residual)
            image = operate(precon)
            gamma_next, delta = paired(residual, precon, image)
            ratio = gamma_next / gamma
            alpha = gamma_next / (delta - ratio * gamma_next / alpha)
            direction = precon + spread(ratio) * direction
            along = image + spread(ratio) * along
            gamma = gamma_next
    return (solution, residual)


def solution(mesh):
    placed = (
        P(("case", "gx"), "gy", None, None),
        P(None, ("case", "gx"), "gy", None, None),
        P(None, ("case", "gx"), "gy"),
        P(("case", "gx"), "gy", None),
    )
    return jax.shard_map(
        local,
        mesh=mesh,
        in_specs=placed,
        out_specs=(P(("case", "gx"), "gy", None, None), P(("case", "gx"), "gy", None, None)),
        check_vma=False,
    )
```

profile of v0, /device:TPU:0, one launch (start us, length us, event | category | flops | bytes accessed | tf_op | source)
XLA Modules:
  0.0 493.8 jit_solution(1748512622041219275)
XLA Ops:
  3.5 5.1 %collective-permute-start = (f32[4,1,6,128,128]{3,4,2,0,1:T(8,128)S(1)}, f32[4,1,6,128,128]{3,4,2,0,1:T(8,128)S(1)}, u32[]{:S(2)}, u32[]{:S(2)}) collective-permute-start(f32[4,1,6,128,128]{3,4,2,0,1:T(8,128)S(1)} %bitcast.499), channel_id=1, source_target_pairs={{0,4},{1,5},{2,6},{3,7},{8,12},{9,13},{10,14},{11,15},{16,20},{17,... | collective-permute-start | bytes 4718600 | tf_op jit(solution)/shard_map/ppermute | solution.py:22
  9.9 32.1 %collective-permute-done = f32[4,1,6,128,128]{3,4,2,0,1:T(8,128)S(1)} collective-permute-done((f32[4,1,6,128,128]{3,4,2,0,1:T(8,128)S(1)}, f32[4,1,6,128,128]{3,4,2,0,1:T(8,128)S(1)}, u32[]{:S(2)}, u32[]{:S(2)}) %collective-permute-start) | collective-permute-done | bytes 1572896 | tf_op jit(solution)/shard_map/ppermute | solution.py:22
  42.0 4.2 collective-permute-done.1
  63.1 71.1 %custom-call.11 = f32[6,128,128]{2,1,0:T(8,128)S(1)} custom-call(f32[6,128,128]{2,1,0:T(8,128)} %fusion.15), custom_call_target="Cholesky" | custom-call | tf_op jit(solution)/shard_map/jit(cholesky)/cholesky | solution.py:61
  136.0 59.8 %custom-call.12 = f32[6,1,128,128]{2,3,1,0:T(8,128)S(1)} custom-call(f32[6,1,128,128]{3,2,1,0:T(8,128)} %select_bitcast_fusion), custom_call_target="InvertDiagBlocksLowerTriangular" | custom-call | tf_op jit(solution)/shard_map/vmap(jit(_cho_solve))/triangular_solve | solution.py:62
  202.2 4.6 collective-permute-start.5
  210.6 11.7 %collective-permute-start.7 = (f32[3,1,32,128]{3,2,1,0:T(8,128)S(1)}, f32[3,1,32,128]{3,2,1,0:T(8,128)S(1)}, u32[]{:S(2)}, u32[]{:S(2)}) collective-permute-start(f32[3,1,32,128]{3,2,1,0:T(8,128)S(1)} %get-tuple-element.64), channel_id=1, source_target_pairs={{0,1},{1,2},{2,3},{4,5},{5,6},{6,7},{8,9},{9,10},{10,11},{12,13},{... | collective-permute-start | bytes 147464 | tf_op jit(solution)/shard_map/ppermute | solution.py:22
  226.0 14.0 %all-reduce.7 = (f32[32]{0:T(128)S(1)}, f32[32]{0:T(128)S(1)}) all-reduce(f32[32]{0:T(128)S(1)} %multiply_reduce_fusion.14, f32[32]{0:T(128)S(1)} %get-tuple-element.68), channel_id=1, replica_groups=mesh['case'=4,'gx'=2,'gy'=4] {'gx','gy'}, use_global_device_ids=true, to_apply=%region_4.5 | all-reduce | flops 64 | bytes 512 | tf_op jit(solution)/shard_map/psum | solution.py:90
  244.8 4.6 collective-permute-start.9
  259.8 14.8 %all-reduce.6 = (f32[32]{0:T(128)S(1)}, f32[32]{0:T(128)}) all-reduce(f32[32]{0:T(128)S(1)} %get-tuple-element.70, f32[32]{0:T(128)S(1)} %get-tuple-element.72), channel_id=1, replica_groups=mesh['case'=4,'gx'=2,'gy'=4] {'gx','gy'}, use_global_device_ids=true, to_apply=%region_8.9 | all-reduce | flops 64 | bytes 512 | tf_op jit(solution)/shard_map/psum | solution.py:90
  280.6 4.6 collective-permute-start.13
  296.1 13.8 %all-reduce.5 = (f32[32]{0:T(128)S(1)}, f32[32]{0:T(128)}) all-reduce(f32[32]{0:T(128)} %get-tuple-element.74, f32[32]{0:T(128)} %get-tuple-element.76), channel_id=1, replica_groups=mesh['case'=4,'gx'=2,'gy'=4] {'gx','gy'}, use_global_device_ids=true, to_apply=%region_12.13 | all-reduce | flops 64 | bytes 512 | tf_op jit(solution)/shard_map/psum | solution.py:90
  316.7 4.6 collective-permute-start.17
  331.7 14.5 %all-reduce.4 = (f32[32]{0:T(128)S(1)}, f32[32]{0:T(128)}) all-reduce(f32[32]{0:T(128)} %get-tuple-element.78, f32[32]{0:T(128)S(1)} %get-tuple-element.80), channel_id=1, replica_groups=mesh['case'=4,'gx'=2,'gy'=4] {'gx','gy'}, use_global_device_ids=true, to_apply=%region_16.17 | all-reduce | flops 64 | bytes 512 | tf_op jit(solution)/shard_map/psum | solution.py:90
  352.7 4.6 collective-permute-start.21
  368.2 13.9 %all-reduce.3 = (f32[32]{0:T(128)S(1)}, f32[32]{0:T(128)}) all-reduce(f32[32]{0:T(128)} %get-tuple-element.82, f32[32]{0:T(128)} %get-tuple-element.84), channel_id=1, replica_groups=mesh['case'=4,'gx'=2,'gy'=4] {'gx','gy'}, use_global_device_ids=true, to_apply=%region_20.21 | all-reduce | flops 64 | bytes 512 | tf_op jit(solution)/shard_map/psum | solution.py:90
  388.9 4.6 collective-permute-start.25
  403.9 14.3 %all-reduce.2 = (f32[32]{0:T(128)}, f32[32]{0:T(128)}) all-reduce(f32[32]{0:T(128)} %get-tuple-element.86, f32[32]{0:T(128)S(1)} %get-tuple-element.88), channel_id=1, replica_groups=mesh['case'=4,'gx'=2,'gy'=4] {'gx','gy'}, use_global_device_ids=true, to_apply=%region_24.25 | all-reduce | flops 64 | bytes 512 | tf_op jit(solution)/shard_map/psum | solution.py:90
  423.6 4.6 collective-permute-start.29
  435.7 3.5 multiply_reduce_fusion.2
  439.2 14.0 %all-reduce.1 = (f32[32]{0:T(128)}, f32[32]{0:T(128)}) all-reduce(f32[32]{0:T(128)S(1)} %multiply_reduce_fusion.3, f32[32]{0:T(128)} %get-tuple-element.92), channel_id=1, replica_groups=mesh['case'=4,'gx'=2,'gy'=4] {'gx','gy'}, use_global_device_ids=true, to_apply=%region_28.29 | all-reduce | flops 64 | bytes 512 | tf_op jit(solution)/shard_map/psum | solution.py:90
  459.4 4.6 collective-permute-start.33
  471.4 3.5 multiply_reduce_fusion
  474.9 13.9 %all-reduce = (f32[32]{0:T(128)S(1)}, f32[32]{0:T(128)S(1)}) all-reduce(f32[32]{0:T(128)} %get-tuple-element.94, f32[32]{0:T(128)} %get-tuple-element.96), channel_id=1, replica_groups=mesh['case'=4,'gx'=2,'gy'=4] {'gx','gy'}, use_global_device_ids=true, to_apply=%region_32.33 | all-reduce | flops 64 | bytes 512 | tf_op jit(solution)/shard_map/psum | solution.py:90
  (289 shorter events, 150.6 us)
Async XLA Ops:
  3.5 38.5 %collective-permute-start = (f32[4,1,6,128,128]{3,4,2,0,1:T(8,128)S(1)}, f32[4,1,6,128,128]{3,4,2,0,1:T(8,128)S(1)}, u32[]{:S(2)}, u32[]{:S(2)}) collective-permute-start(f32[4,1,6,128,128]{3,4,2,0,1:T(8,128)S(1)} %bitcast.499), channel_id=1, source_target_pairs={{0,4},{1,5},{2,6},{3,7},{8,12},{9,13},{10,14},{11,15},{16,20},{17,... | collective-permute-start | bytes 4718600 | tf_op jit(solution)/shard_map/ppermute | solution.py:22
  8.6 37.6 %collective-permute-start.1 = (f32[4,1,6,128,128]{3,4,2,0,1:T(8,128)S(1)}, f32[4,1,6,128,128]{3,4,2,0,1:T(8,128)S(1)}, u32[]{:S(2)}, u32[]{:S(2)}) collective-permute-start(f32[4,1,6,128,128]{3,4,2,0,1:T(8,128)S(1)} %bitcast.500), channel_id=1, source_target_pairs={{4,0},{5,1},{6,2},{7,3},{12,8},{13,9},{14,10},{15,11},{20,16},{21,... | collective-permute-start | bytes 4718600 | tf_op jit(solution)/shard_map/ppermute | solution.py:24
  47.8 5.2 %collective-permute-start.2 = (f32[4,3,1,128,128]{3,4,2,0,1:T(8,128)}, f32[4,3,1,128,128]{3,4,2,0,1:T(8,128)}, u32[]{:S(2)}, u32[]{:S(2)}) collective-permute-start(f32[4,3,1,128,128]{3,4,2,0,1:T(8,128)} %get-tuple-element.46), channel_id=1, source_target_pairs={{0,1},{1,2},{2,3},{4,5},{5,6},{6,7},{8,9},{9,10},{10,11},{12,13},{... | collective-permute-start | bytes 2359304 | tf_op jit(solution)/shard_map/ppermute | solution.py:22
  50.0 5.5 %collective-permute-start.3 = (f32[4,3,1,128,128]{3,4,2,0,1:T(8,128)}, f32[4,3,1,128,128]{3,4,2,0,1:T(8,128)}, u32[]{:S(2)}, u32[]{:S(2)}) collective-permute-start(f32[4,3,1,128,128]{3,4,2,0,1:T(8,128)} %get-tuple-element.47), channel_id=1, source_target_pairs={{1,0},{2,1},{3,2},{5,4},{6,5},{7,6},{9,8},{10,9},{11,10},{13,12},{... | collective-permute-start | bytes 2359304 | tf_op jit(solution)/shard_map/ppermute | solution.py:24
  200.7 8.5 %collective-permute-start.4 = (f32[1,6,32,128]{3,2,1,0:T(8,128)S(1)}, f32[1,6,32,128]{3,2,1,0:T(8,128)S(1)}, u32[]{:S(2)}, u32[]{:S(2)}) collective-permute-start(f32[1,6,32,128]{3,2,1,0:T(8,128)S(1)} %bitcast.503), channel_id=1, source_target_pairs={{4,0},{5,1},{6,2},{7,3},{12,8},{13,9},{14,10},{15,11},{20,16},{21,... | collective-permute-start | bytes 294920 | tf_op jit(solution)/shard_map/ppermute | solution.py:24
  202.2 7.1 %collective-permute-start.5 = (f32[1,6,32,128]{3,2,1,0:T(8,128)S(1)}, f32[1,6,32,128]{3,2,1,0:T(8,128)S(1)}, u32[]{:S(2)}, u32[]{:S(2)}) collective-permute-start(f32[1,6,32,128]{3,2,1,0:T(8,128)S(1)} %bitcast.504), channel_id=1, source_target_pairs={{0,4},{1,5},{2,6},{3,7},{8,12},{9,13},{10,14},{11,15},{16,20},{17,... | collective-permute-start | bytes 294920 | tf_op jit(solution)/shard_map/ppermute | solution.py:22
  209.3 13.1 %collective-permute-start.6 = (f32[3,1,32,128]{3,2,1,0:T(8,128)S(1)}, f32[3,1,32,128]{3,2,1,0:T(8,128)S(1)}, u32[]{:S(2)}, u32[]{:S(2)}) collective-permute-start(f32[3,1,32,128]{3,2,1,0:T(8,128)S(1)} %get-tuple-element.65), channel_id=1, source_target_pairs={{1,0},{2,1},{3,2},{5,4},{6,5},{7,6},{9,8},{10,9},{11,10},{13,12},{... | collective-permute-start | bytes 147464 | tf_op jit(solution)/shard_map/ppermute | solution.py:24
  210.6 12.4 %collective-permute-start.7 = (f32[3,1,32,128]{3,2,1,0:T(8,128)S(1)}, f32[3,1,32,128]{3,2,1,0:T(8,128)S(1)}, u32[]{:S(2)}, u32[]{:S(2)}) collective-permute-start(f32[3,1,32,128]{3,2,1,0:T(8,128)S(1)} %get-tuple-element.64), channel_id=1, source_target_pairs={{0,1},{1,2},{2,3},{4,5},{5,6},{6,7},{8,9},{9,10},{10,11},{12,13},{... | collective-permute-start | bytes 147464 | tf_op jit(solution)/shard_map/ppermute | solution.py:22
  243.5 6.6 %collective-permute-start.8 = (f32[1,6,32,128]{3,2,1,0:T(8,128)S(1)}, f32[1,6,32,128]{3,2,1,0:T(8,128)S(1)}, u32[]{:S(2)}, u32[]{:S(2)}) collective-permute-start(f32[1,6,32,128]{3,2,1,0:T(8,128)S(1)} %bitcast.512), channel_id=1, source_target_pairs={{4,0},{5,1},{6,2},{7,3},{12,8},{13,9},{14,10},{15,11},{20,16},{21,... | collective-permute-start | bytes 294920 | tf_op jit(solution)/shard_map/ppermute | solution.py:24
  244.8 6.8 %collective-permute-start.9 = (f32[1,6,32,128]{3,2,1,0:T(8,128)S(1)}, f32[1,6,32,128]{3,2,1,0:T(8,128)S(1)}, u32[]{:S(2)}, u32[]{:S(2)}) collective-permute-start(f32[1,6,32,128]{3,2,1,0:T(8,128)S(1)} %bitcast.513), channel_id=1, source_target_pairs={{0,4},{1,5},{2,6},{3,7},{8,12},{9,13},{10,14},{11,15},{16,20},{17,... | collective-permute-start | bytes 294920 | tf_op jit(solution)/shard_map/ppermute | solution.py:22
  279.3 6.5 %collective-permute-start.12 = (f32[1,6,32,128]{3,2,1,0:T(8,128)S(1)}, f32[1,6,32,128]{3,2,1,0:T(8,128)S(1)}, u32[]{:S(2)}, u32[]{:S(2)}) collective-permute-start(f32[1,6,32,128]{3,2,1,0:T(8,128)S(1)} %bitcast.521), channel_id=1, source_target_pairs={{4,0},{5,1},{6,2},{7,3},{12,8},{13,9},{14,10},{15,11},{20,16},{21,... | collective-permute-start | bytes 294920 | tf_op jit(solution)/shard_map/ppermute | solution.py:24
  280.6 6.8 %collective-permute-start.13 = (f32[1,6,32,128]{3,2,1,0:T(8,128)S(1)}, f32[1,6,32,128]{3,2,1,0:T(8,128)S(1)}, u32[]{:S(2)}, u32[]{:S(2)}) collective-permute-start(f32[1,6,32,128]{3,2,1,0:T(8,128)S(1)} %bitcast.522), channel_id=1, source_target_pairs={{0,4},{1,5},{2,6},{3,7},{8,12},{9,13},{10,14},{11,15},{16,20},{17,... | collective-permute-start | bytes 294920 | tf_op jit(solution)/shard_map/ppermute | solution.py:22
  315.4 6.9 %collective-permute-start.16 = (f32[1,6,32,128]{3,2,1,0:T(8,128)S(1)}, f32[1,6,32,128]{3,2,1,0:T(8,128)S(1)}, u32[]{:S(2)}, u32[]{:S(2)}) collective-permute-start(f32[1,6,32,128]{3,2,1,0:T(8,128)S(1)} %bitcast.530), channel_id=1, source_target_pairs={{4,0},{5,1},{6,2},{7,3},{12,8},{13,9},{14,10},{15,11},{20,16},{21,... | collective-permute-start | bytes 294920 | tf_op jit(solution)/shard_map/ppermute | solution.py:24
  316.7 6.8 %collective-permute-start.17 = (f32[1,6,32,128]{3,2,1,0:T(8,128)S(1)}, f32[1,6,32,128]{3,2,1,0:T(8,128)S(1)}, u32[]{:S(2)}, u32[]{:S(2)}) collective-permute-start(f32[1,6,32,128]{3,2,1,0:T(8,128)S(1)} %bitcast.531), channel_id=1, source_target_pairs={{0,4},{1,5},{2,6},{3,7},{8,12},{9,13},{10,14},{11,15},{16,20},{17,... | collective-permute-start | bytes 294920 | tf_op jit(solution)/shard_map/ppermute | solution.py:22
  323.5 4.6 collective-permute-start.18
  351.4 6.6 %collective-permute-start.20 = (f32[1,6,32,128]{3,2,1,0:T(8,128)S(1)}, f32[1,6,32,128]{3,2,1,0:T(8,128)S(1)}, u32[]{:S(2)}, u32[]{:S(2)}) collective-permute-start(f32[1,6,32,128]{3,2,1,0:T(8,128)S(1)} %bitcast.539), channel_id=1, source_target_pairs={{4,0},{5,1},{6,2},{7,3},{12,8},{13,9},{14,10},{15,11},{20,16},{21,... | collective-permute-start | bytes 294920 | tf_op jit(solution)/shard_map/ppermute | solution.py:24
  352.7 6.8 %collective-permute-start.21 = (f32[1,6,32,128]{3,2,1,0:T(8,128)S(1)}, f32[1,6,32,128]{3,2,1,0:T(8,128)S(1)}, u32[]{:S(2)}, u32[]{:S(2)}) collective-permute-start(f32[1,6,32,128]{3,2,1,0:T(8,128)S(1)} %bitcast.540), channel_id=1, source_target_pairs={{0,4},{1,5},{2,6},{3,7},{8,12},{9,13},{10,14},{11,15},{16,20},{17,... | collective-permute-start | bytes 294920 | tf_op jit(solution)/shard_map/ppermute | solution.py:22
  387.6 6.8 %collective-permute-start.24 = (f32[1,6,32,128]{3,2,1,0:T(8,128)S(1)}, f32[1,6,32,128]{3,2,1,0:T(8,128)S(1)}, u32[]{:S(2)}, u32[]{:S(2)}) collective-permute-start(f32[1,6,32,128]{3,2,1,0:T(8,128)S(1)} %bitcast.548), channel_id=1, source_target_pairs={{4,0},{5,1},{6,2},{7,3},{12,8},{13,9},{14,10},{15,11},{20,16},{21,... | collective-permute-start | bytes 294920 | tf_op jit(solution)/shard_map/ppermute | solution.py:24
  388.9 6.8 %collective-permute-start.25 = (f32[1,6,32,128]{3,2,1,0:T(8,128)S(1)}, f32[1,6,32,128]{3,2,1,0:T(8,128)S(1)}, u32[]{:S(2)}, u32[]{:S(2)}) collective-permute-start(f32[1,6,32,128]{3,2,1,0:T(8,128)S(1)} %bitcast.549), channel_id=1, source_target_pairs={{0,4},{1,5},{2,6},{3,7},{8,12},{9,13},{10,14},{11,15},{16,20},{17,... | collective-permute-start | bytes 294920 | tf_op jit(solution)/shard_map/ppermute | solution.py:22
  422.3 6.6 %collective-permute-start.28 = (f32[1,6,32,128]{3,2,1,0:T(8,128)S(1)}, f32[1,6,32,128]{3,2,1,0:T(8,128)S(1)}, u32[]{:S(2)}, u32[]{:S(2)}) collective-permute-start(f32[1,6,32,128]{3,2,1,0:T(8,128)S(1)} %bitcast.557), channel_id=1, source_target_pairs={{4,0},{5,1},{6,2},{7,3},{12,8},{13,9},{14,10},{15,11},{20,16},{21,... | collective-permute-start | bytes 294920 | tf_op jit(solution)/shard_map/ppermute | solution.py:24
  423.6 6.8 %collective-permute-start.29 = (f32[1,6,32,128]{3,2,1,0:T(8,128)S(1)}, f32[1,6,32,128]{3,2,1,0:T(8,128)S(1)}, u32[]{:S(2)}, u32[]{:S(2)}) collective-permute-start(f32[1,6,32,128]{3,2,1,0:T(8,128)S(1)} %bitcast.558), channel_id=1, source_target_pairs={{0,4},{1,5},{2,6},{3,7},{8,12},{9,13},{10,14},{11,15},{16,20},{17,... | collective-permute-start | bytes 294920 | tf_op jit(solution)/shard_map/ppermute | solution.py:22
  430.4 4.6 collective-permute-start.30
  458.1 6.8 %collective-permute-start.32 = (f32[1,6,32,128]{3,2,1,0:T(8,128)S(1)}, f32[1,6,32,128]{3,2,1,0:T(8,128)S(1)}, u32[]{:S(2)}, u32[]{:S(2)}) collective-permute-start(f32[1,6,32,128]{3,2,1,0:T(8,128)S(1)} %bitcast.566), channel_id=1, source_target_pairs={{4,0},{5,1},{6,2},{7,3},{12,8},{13,9},{14,10},{15,11},{20,16},{21,... | collective-permute-start | bytes 294920 | tf_op jit(solution)/shard_map/ppermute | solution.py:24
  459.4 6.8 %collective-permute-start.33 = (f32[1,6,32,128]{3,2,1,0:T(8,128)S(1)}, f32[1,6,32,128]{3,2,1,0:T(8,128)S(1)}, u32[]{:S(2)}, u32[]{:S(2)}) collective-permute-start(f32[1,6,32,128]{3,2,1,0:T(8,128)S(1)} %bitcast.567), channel_id=1, source_target_pairs={{0,4},{1,5},{2,6},{3,7},{8,12},{9,13},{10,14},{11,15},{16,20},{17,... | collective-permute-start | bytes 294920 | tf_op jit(solution)/shard_map/ppermute | solution.py:22
  (59 other events, 489.1 us)
where the time goes:
time: 504 us; the launch traced here: 494 us
  other arithmetic  162 us (32%)
  blocking collectives  113 us (22%)
  starting transfers between devices  100 us (20%)
  waiting for transfers between devices  59.8 us (12%)
  matrix products  47.7 us (9%)
  local copies, waits for them, and re-layouts  8.54 us (2%)
    psum x8, blocking collectives, paired(): lax.psum((inner(residual, precon), inner(image, precon)), ('gx', 'gy'))  113 us
    ppermute x18, starting transfers between devices, extended(): lax.ppermute(tail, axis, [(i, (i + 1) % count) for i in range(ends)])  77.2 us
    another operation x4, other arithmetic, local(): lower = jnp.linalg.cholesky(diagonal.reshape(-1, B, B))  72.6 us
    another operation x3, other arithmetic, local(): jax.scipy.linalg.cho_solve((factor, True), identity)  60.7 us
    ppermute x18, waiting for transfers between devices, extended(): lax.ppermute(tail, axis, [(i, (i + 1) % count) for i in range(ends)])  47.4 us
    dot_general x8, matrix products, operate(): jnp.einsum('kxyab,kxyrb->xyra', blocks, jnp.stack(pieces), precision=PREC...  25.5 us
    ppermute x18, starting transfers between devices, extended(): lax.ppermute(head, axis, [((i + 1) % count, i) for i in range(ends)])  23.2 us
    dot_general x8, matrix products, precondition(): jnp.einsum('xyab,xyrb->xyra', inverse, field, precision=PRECISE, preferre...  16.8 us
  transfers between devices with their start and end apart: 36, of which 25 were waited for; matrix products, arithmetic and copies ran while one was open for 1% of the time, Pallas kernels for 0%

commit v1 on v0

--- a/solution.py
+++ b/solution.py
@@ -1,6 +1,8 @@
 import jax
 import jax.numpy as jnp
 from jax import lax
+from jax.experimental import pallas as pl
+from jax.experimental.pallas import tpu as pltpu
 from jax.sharding import PartitionSpec as P
 
 B = 128
@@ -40,7 +42,7 @@
     return values[None, None, :, None]
 
 
-def local(load, factors, links, shift):
+def local_halo(load, factors, links, shift):
     count_x, count_y = (load.shape[0], load.shape[1])
     masked = factors * links.astype(jnp.bfloat16)[:, :, :, None, None]
     springs = (
@@ -111,6 +113,242 @@
     return (solution, residual)
 
 
+GRID_AXES = ("gx", "gy")
+ROWS = 4
+VMEM = pl.BlockSpec(memory_space=pltpu.VMEM)
+VMEM_BYTES = 56 * 1024 * 1024
+
+
+def gram(block):
+    return (
+        lax.dot_general(block, block, (((1,), (1,)), ((), ())), preferred_element_type=jnp.float32)
+        / B
+    )
+
+
+def split(value):
+    first = value.astype(jnp.bfloat16)
+    rest = value - first.astype(jnp.float32)
+    second = rest.astype(jnp.bfloat16)
+    third = (rest - second.astype(jnp.float32)).astype(jnp.bfloat16)
+    return first, second, third
+
+
+def invert_kernel(ahead, behind, shift, out, work):
+    nodes = shift.shape[0]
+    rows = lax.broadcasted_iota(jnp.int32, (B, B), 0)
+    lanes = lax.broadcasted_iota(jnp.int32, (B, B), 1)
+    for node in range(nodes):
+        total = jnp.where(rows == lanes, shift[pl.ds(node, 1), :], 0.0)
+        for d in range(len(OFFSETS)):
+            total = total + gram(ahead[d, node])
+            total = total + gram(behind[d, node])
+        work[node] = total
+
+    def step(k, carry):
+        lane = lax.broadcasted_iota(jnp.int32, (1, B), 1)
+        for node in range(nodes):
+            block = work[node]
+            row = work[node, pl.ds(k, 1), :]
+            column = jnp.take_along_axis(block, jnp.full((B, B), k, jnp.int32), axis=1)
+            pivot = jnp.sum(jnp.where(lane == k, row, 0.0), axis=1, keepdims=True)
+            scaled = jnp.where(lane == k, 1.0, row) / pivot
+            work[node] = jnp.where(lanes == k, 0.0, block) - column * scaled
+            work[node, pl.ds(k, 1), :] = scaled
+        return carry
+
+    lax.fori_loop(0, B, step, 0)
+    for node in range(nodes):
+        out[node] = work[node]
+
+
+def invert(ahead, behind, shift):
+    nodes = shift.shape[0]
+    return pl.pallas_call(
+        invert_kernel,
+        out_shape=jax.ShapeDtypeStruct((nodes, B, B), jnp.float32),
+        in_specs=[VMEM] * 3,
+        out_specs=VMEM,
+        scratch_shapes=[pltpu.VMEM((nodes, B, B), jnp.float32)],
+    )(ahead, behind, shift)
+
+
+def stacked(value):
+    first, second, third = (term.astype(jnp.float32) for term in split(value))
+    upper = lax.broadcasted_iota(jnp.int32, value.shape, 0) < ROWS
+    both = [jnp.where(upper, first, second), jnp.where(upper, third, 0.0)]
+    return jnp.concatenate(both, axis=0).astype(jnp.bfloat16)
+
+
+def product(left, right):
+    full = jnp.dot(left, right, preferred_element_type=jnp.float32)
+    total = full[: 2 * ROWS, :B] + full[2 * ROWS :, :B]
+    for part in range(1, right.shape[1] // B):
+        total = total + full[: 2 * ROWS, part * B : (part + 1) * B]
+    return total + jnp.concatenate([total[ROWS:], total[:ROWS]], axis=0)
+
+
+def solve_kernel(nx, ny, nbx, nby):
+    ncy = ny // nby
+    devices = (nx // nbx) * ncy
+    unroll = 2 if ny % 2 == 0 else 1
+
+    def kernel(load, shift, factors, inverse, out_x, out_r, w, m, p, q, image, x, r, z, mass):
+        def prepare(dev, carry):
+            for lx in range(nbx):
+                for ly in range(nby):
+                    gx, gy = (dev // ncy) * nbx + lx, (dev % ncy) * nby + ly
+                    node = lx * nby + ly
+                    for d in range(len(OFFSETS)):
+                        first, second, _ = split(gram(factors[dev, d, node]))
+                        w[d, gx, gy, :, :B] = first
+                        w[d, gx, gy, :, B:] = second
+                    for part, term in enumerate(split(inverse[dev, node])):
+                        m[gx, gy, :, part * B : (part + 1) * B] = term
+                    field = load[dev, node]
+                    r[gx, gy] = jnp.concatenate([field, field], axis=0)
+                    mass[gx, gy] = jnp.broadcast_to(shift[dev, pl.ds(node, 1), :], (2 * ROWS, B))
+            return carry
+
+        lax.fori_loop(0, devices, prepare, 0)
+        p[...] = jnp.zeros_like(p)
+        q[...] = jnp.zeros_like(q)
+        x[...] = jnp.zeros_like(x)
+        zero = jnp.zeros((2 * ROWS, B), jnp.float32)
+
+        def total(values):
+            return jnp.sum(values, axis=1, keepdims=True)
+
+        def iterate(_, rz_old):
+            def precondition(y, acc):
+                for i in range(nx):
+                    value = r[i, y]
+                    precon = product(stacked(value), m[i, y])
+                    z[i, y] = precon
+                    acc = acc + value * precon
+                return acc
+
+            rz = total(lax.fori_loop(0, ny, precondition, zero, unroll=2 * unroll))
+            ratio = rz / rz_old
+
+            def advance(y, carry):
+                for i in range(nx):
+                    p[1 + i, 1 + y] = z[i, y] + ratio * p[1 + i, 1 + y]
+                return carry
+
+            lax.fori_loop(0, ny, advance, 0, unroll=2 * unroll)
+
+            def edges(y, carry):
+                for i in range(nx):
+                    for d, (step_x, step_y) in enumerate(OFFSETS):
+                        delta = p[1 + i, 1 + y] - p[1 + i + step_x, 1 + y + step_y]
+                        q[d, 1 + i, 1 + y] = product(stacked(delta), w[d, i, y])
+                return carry
+
+            lax.fori_loop(0, ny, edges, 0, unroll=unroll)
+
+            def gather(y, acc):
+                for i in range(nx):
+                    value = p[1 + i, 1 + y]
+                    result = mass[i, y] * value
+                    for d, (step_x, step_y) in enumerate(OFFSETS):
+                        result = result + (
+                            q[d, 1 + i, 1 + y] - q[d, 1 + i - step_x, 1 + y - step_y]
+                        )
+                    image[i, y] = result
+                    acc = acc + value * result
+                return acc
+
+            alpha = rz / total(lax.fori_loop(0, ny, gather, zero, unroll=2 * unroll))
+
+            def update(y, carry):
+                for i in range(nx):
+                    x[i, y] = x[i, y] + alpha * p[1 + i, 1 + y]
+                    r[i, y] = r[i, y] - alpha * image[i, y]
+                return carry
+
+            lax.fori_loop(0, ny, update, 0, unroll=2 * unroll)
+            return rz
+
+        lax.fori_loop(0, ITERS, iterate, jnp.ones((2 * ROWS, 1), jnp.float32))
+
+        def finish(dev, carry):
+            for lx in range(nbx):
+                for ly in range(nby):
+                    gx, gy = (dev // ncy) * nbx + lx, (dev % ncy) * nby + ly
+                    out_x[dev, lx * nby + ly] = x[gx, gy][:ROWS]
+                    out_r[dev, lx * nby + ly] = r[gx, gy][:ROWS]
+            return carry
+
+        lax.fori_loop(0, devices, finish, 0)
+
+    return kernel
+
+
+def solve(load, shift, factors, inverse, nx, ny, nbx, nby):
+    tall = 2 * ROWS
+    field = pltpu.VMEM((nx, ny, tall, B), jnp.float32)
+    return pl.pallas_call(
+        solve_kernel(nx, ny, nbx, nby),
+        out_shape=[jax.ShapeDtypeStruct(load.shape, jnp.float32)] * 2,
+        in_specs=[VMEM] * 4,
+        out_specs=[VMEM] * 2,
+        scratch_shapes=[
+            pltpu.VMEM((len(OFFSETS), nx, ny, B, 2 * B), jnp.bfloat16),
+            pltpu.VMEM((nx, ny, B, 3 * B), jnp.bfloat16),
+            pltpu.VMEM((nx + 2, ny + 2, tall, B), jnp.float32),
+            pltpu.VMEM((len(OFFSETS), nx + 2, ny + 2, tall, B), jnp.float32),
+        ]
+        + [field] * 5,
+        compiler_params=pltpu.CompilerParams(vmem_limit_bytes=VMEM_BYTES),
+    )(load, shift, factors, inverse)
+
+
+def shifted(cells, axis, dim, step):
+    count = lax.axis_size(axis)
+    size = cells.shape[dim]
+    if step == 1:
+        rim = lax.slice_in_dim(cells, size - 1, size, axis=dim)
+        rim = lax.ppermute(rim, axis, [(i, i + 1) for i in range(count - 1)])
+        return jnp.concatenate([rim, lax.slice_in_dim(cells, 0, size - 1, axis=dim)], axis=dim)
+    rim = lax.slice_in_dim(cells, 0, 1, axis=dim)
+    rim = lax.ppermute(rim, axis, [(i + 1, i) for i in range(count - 1)])
+    return jnp.concatenate([lax.slice_in_dim(cells, 1, size, axis=dim), rim], axis=dim)
+
+
+def local_columns(load, factors, links, shift):
+    nbx, nby, rhs, _ = load.shape
+    gx, gy = (lax.axis_size(axis) for axis in GRID_AXES)
+    devices, nodes = gx * gy, nbx * nby
+    masked = factors * links.astype(jnp.bfloat16)[:, :, :, None, None]
+    gathered = lax.all_gather(masked.reshape(4, nodes, B, B), GRID_AXES)
+    down = shifted(jnp.stack([masked[0], masked[2], masked[3]]), "gx", 1, 1)
+    left = shifted(jnp.stack([masked[1], down[1]]), "gy", 2, 1)
+    right = shifted(down[2:], "gy", 2, -1)
+    behind = jnp.stack([down[0], left[0], left[1], right[0]])
+    flat_shift = shift.reshape(nodes, B)
+    inverse = invert(
+        masked.reshape(4, nodes, B, B), behind.reshape(4, nodes, B, B), flat_shift
+    )
+    columns = load.reshape(nodes, devices, ROWS, B).transpose(1, 0, 2, 3)
+    columns = lax.all_to_all(columns, GRID_AXES, 0, 0)
+    shifts = lax.all_gather(flat_shift, GRID_AXES)
+    inverses = lax.all_gather(inverse, GRID_AXES)
+    outs = solve(columns, shifts, gathered, inverses, gx * nbx, gy * nby, nbx, nby)
+    outs = lax.all_to_all(jnp.stack(outs, axis=1), GRID_AXES, 0, 0)
+    outs = outs.transpose(1, 2, 0, 3, 4).reshape(2, nbx, nby, rhs, B)
+    return (outs[0], outs[1])
+
+
+def local(load, factors, links, shift):
+    devices = lax.axis_size("gx") * lax.axis_size("gy")
+    blocks = devices * load.shape[0] * load.shape[1]
+    held = blocks * B * B * (len(OFFSETS) * 6 + 10)
+    if load.shape[2] == ROWS * devices and held < VMEM_BYTES * 3 // 4:
+        return local_columns(load, factors, links, shift)
+    return local_halo(load, factors, links, shift)
+
+
 def solution(mesh):
     placed = (
         P(("case", "gx"), "gy", None, None),

time: 504 us -> 275 us (0.55); the launches traced: 494 us -> 275 us
  other arithmetic: 162 us -> 7.19 us
  Pallas kernels: 0 us -> 140 us
  blocking collectives: 113 us -> 19.5 us
  starting transfers between devices: 100 us -> 14.4 us
  matrix products: 47.7 us -> 0 us
  waiting for transfers between devices: 59.8 us -> 77.2 us
  between operations: 2.51 us -> 14.2 us
  local copies, waits for them, and re-layouts: 8.54 us -> 2.72 us
    pallas_call x0 -> x2, Pallas kernels: none -> 140 us  [the longest x1 88.3 us: invert(): pl.pallas_call(invert_kernel, out_shape=jax.ShapeDtypeStruct((nodes, B, B...]
    another operation x15 -> x2, other arithmetic: 133 us -> 1.04 us  [the longest x1 0.99 us: local_columns(): outs = lax.all_to_all(jnp.stack(outs, axis=1), GRID_AXES, 0, 0)]
    psum x8 -> x0, blocking collectives: 113 us -> none  [paired(): lax.psum((inner(residual, precon), inner(image, precon)), ('gx', 'gy'))]
    ppermute x36 -> x3, starting transfers between devices: 100 us -> 9.25 us  [the longest x2 7.97 us: shifted(): rim = lax.ppermute(rim, axis, [(i, i + 1) for i in range(count - 1)])]
    all_gather x0 -> x2, waiting for transfers between devices: none -> 64.7 us  [the longest x1 47.3 us: local_columns(): gathered = lax.all_gather(masked.reshape(4, nodes, B, B), GRID_AXES)]
    ppermute x36 -> x3, waiting for transfers between devices: 59.8 us -> 12.5 us  [the longest x2 12.5 us: shifted(): rim = lax.ppermute(rim, axis, [(i, i + 1) for i in range(count - 1)])]
    dot_general x17 -> x0, matrix products: 44.4 us -> none  [the longest x8 25.5 us: operate(): jnp.einsum('kxyab,kxyrb->xyra', blocks, jnp.stack(pieces), precision=PREC...]
    all_gather x0 -> x1, blocking collectives: none -> 10.8 us  [local_columns(): shifts = lax.all_gather(flat_shift, GRID_AXES)]
  transfers between devices with their start and end apart: 36 -> 6, of which waited for: 25 -> 3; matrix products, arithmetic and copies ran while one was open for 1% -> 2% of each run, Pallas kernels for 0% -> 0%
where the time goes in v1:
time: 275 us
  Pallas kernels  140 us (51%)
  waiting for transfers between devices  77.2 us (28%)
  blocking collectives  19.5 us (7%)
  starting transfers between devices  14.4 us (5%)
  between operations  14.2 us (5%)
  other arithmetic  7.19 us (3%)
    pallas_call x1, Pallas kernels, invert(): pl.pallas_call(invert_kernel, out_shape=jax.ShapeDtypeStruct((nodes, B, B...  88.3 us
    pallas_call x1, Pallas kernels, solve(): pl.pallas_call(solve_kernel(nx, ny, nbx, nby), out_shape=[jax.ShapeDtypeS...  51.3 us
    all_gather x1, waiting for transfers between devices, local_columns(): gathered = lax.all_gather(masked.reshape(4, nodes, B, B), GRID_AXES)  47.3 us
    all_gather x1, waiting for transfers between devices, local_columns(): inverses = lax.all_gather(inverse, GRID_AXES)  17.4 us
    ppermute x2, waiting for transfers between devices, shifted(): rim = lax.ppermute(rim, axis, [(i, i + 1) for i in range(count - 1)])  12.5 us
    all_gather x1, blocking collectives, local_columns(): shifts = lax.all_gather(flat_shift, GRID_AXES)  10.8 us
    all_to_all x1, blocking collectives, local_columns(): outs = lax.all_to_all(jnp.stack(outs, axis=1), GRID_AXES, 0, 0)  8.74 us
    ppermute x2, starting transfers between devices, shifted(): rim = lax.ppermute(rim, axis, [(i, i + 1) for i in range(count - 1)])  7.97 us
  transfers between devices with their start and end apart: 6, of which 3 were waited for; matrix products, arithmetic and copies ran while one was open for 2% of the time, Pallas kernels for 0%

profile of v1, /device:TPU:0, one launch (start us, length us, event | category | flops | bytes accessed | tf_op | source)
XLA Modules:
  0.0 274.9 jit_solution(1659622037909437845)
XLA Ops:
  7.2 0.0 all-gather.7.cloned.1.call-start
  7.2 0.7 convert_element_type.3
  8.0 1.2 bitcast_multiply_fusion
  9.3 0.1 pad_maximum_fusion.1
  9.4 4.9 %collective-permute-start = (bf16[3,1,6,128,128]{4,3,2,0,1:T(8,128)(2,1)S(1)}, bf16[3,1,6,128,128]{4,3,2,0,1:T(8,128)(2,1)S(1)}, u32[]{:S(2)}, u32[]{:S(2)}) collective-permute-start(bf16[3,1,6,128,128]{4,3,2,0,1:T(8,128)(2,1)S(1)} %pad_maximum_fusion.1), channel_id=1, source_target_pairs={{0,4},{1,5},{2,6},{3,7},{8,12},{9,13},{10,14},{11,15},{16,20},{17,... | collective-permute-start | bytes 1769480 | tf_op jit(solution)/shard_map/ppermute | solution.py:312
  14.3 12.5 %collective-permute-done = bf16[3,1,6,128,128]{4,3,2,0,1:T(8,128)(2,1)S(1)} collective-permute-done((bf16[3,1,6,128,128]{4,3,2,0,1:T(8,128)(2,1)S(1)}, bf16[3,1,6,128,128]{4,3,2,0,1:T(8,128)(2,1)S(1)}, u32[]{:S(2)}, u32[]{:S(2)}) %collective-permute-start) | collective-permute-done | bytes 589856 | tf_op jit(solution)/shard_map/ppermute | solution.py:312
  26.9 1.3 collective-permute-start.2
  28.2 3.0 %collective-permute-start.1 = (bf16[2,1,1,128,128]{4,3,2,0,1:T(8,128)(2,1)S(1)}, bf16[2,1,1,128,128]{4,3,2,0,1:T(8,128)(2,1)S(1)}, u32[]{:S(2)}, u32[]{:S(2)}) collective-permute-start(bf16[2,1,1,128,128]{4,3,2,0,1:T(8,128)(2,1)S(1)} %pad_maximum_fusion.3), channel_id=1, source_target_pairs={{0,1},{1,2},{2,3},{4,5},{5,6},{6,7},{8,9},{9,10},{10,11},{12,13},{... | collective-permute-start | bytes 196616 | tf_op jit(solution)/shard_map/ppermute | solution.py:312
  31.3 2.1 fusion.7.ahead
  33.4 0.6 copy.28
  34.0 1.0 fusion.3.behind
  35.0 88.3 %shard_map.59 = f32[6,128,128]{2,1,0:T(8,128)} custom-call(bf16[4,6,128,128]{3,2,1,0:T(8,128)(2,1)} %fusion.7.ahead, bf16[4,6,128,128]{3,2,1,0:T(8,128)(2,1)} %fusion.3.behind, f32[6,128]{1,0:T(8,128)} %bitcast.37), custom_call_target="tpu_custom_call" | custom-call | tf_op jit(solution)/shard_map/pallas_call | solution.py:167
  123.4 0.0 all-gather.5.cloned.1.call-start
  123.4 1.0 fusion.8
  124.5 0.7 copy.26
  125.1 5.1 %all-to-all-start = ((f32[8,6,4,128]{3,2,1,0:T(4,128)}), f32[8,6,4,128]{3,2,1,0:T(4,128)S(1)}, u32[]{:S(2)}, u32[]{:S(2)}) async-start(f32[8,6,4,128]{3,2,1,0:T(4,128)} %bitcast.26), calls=%async_computation | async-start | bytes 196608 | tf_op jit(solution)/shard_map/all_to_all | solution.py:334
  130.2 10.8 %all_gather.12.shift = f32[8,6,128]{2,1,0:T(8,128)} all-gather(f32[1,6,128]{2,1,0:T(8,128)S(1)} %copy-done.3), channel_id=1, replica_groups=mesh['case'=4,'gx'=2,'gy'=4] {'gx','gy'}, dimensions={0}, use_global_device_ids=true | all-gather | bytes 27648 | tf_op jit(solution)/shard_map/all_gather | solution.py:335
  141.0 17.4 %all-gather.7.cloned.1.call-done = f32[48,128,128]{2,1,0:T(8,128)} async-done(((f32[6,128,128]{2,1,0:T(8,128)}), f32[48,128,128]{2,1,0:T(8,128)}) %all-gather.7.cloned.1.call-update) | async-done | bytes 3145744 | tf_op jit(solution)/shard_map/all_gather | solution.py:336
  158.3 47.3 %all-gather.5.cloned.1.call-done = bf16[32,1,6,128,128]{4,3,2,1,0:T(8,128)(2,1)} async-done(((bf16[4,1,6,128,128]{4,3,2,1,0:T(8,128)(2,1)}), bf16[32,1,6,128,128]{4,3,2,1,0:T(8,128)(2,1)}) %all-gather.5.cloned.1.call-update) | async-done | bytes 6291472 | tf_op jit(solution)/shard_map/all_gather | solution.py:324
  205.7 51.3 %shard_map.60 = (f32[8,6,4,128]{3,2,1,0:T(4,128)}, f32[8,6,4,128]{3,2,1,0:T(4,128)}) custom-call(f32[8,6,4,128]{3,2,1,0:T(4,128)} %copy-done.1, f32[8,6,128]{2,1,0:T(8,128)} %all_gather.12.shift, bf16[8,4,6,128,128]{4,3,2,1,0:T(8,128)(2,1)} %bitcast.29, f32[8,6,128,128]{3,2,1,0:T(8,128)} %bitcast.30), custom_call_target="tpu_custom_call" | custom-call | tf_op jit(solution)/shard_map/pallas_call | solution.py:291
  256.9 1.0 pad_maximum_fusion.2
  258.0 8.7 %all_to_all.10 = f32[8,2,6,4,128]{4,3,2,1,0:T(4,128)S(1)} all-to-all(f32[8,2,6,4,128]{4,3,2,1,0:T(4,128)S(1)} %copy.17), channel_id=1, replica_groups=mesh['case'=4,'gx'=2,'gy'=4] {'gx','gy'}, dimensions={0} | all-to-all | bytes 393216 | tf_op jit(solution)/shard_map/all_to_all | solution.py:338
  266.7 0.7 copy.19
  267.4 0.7 copy.18
  (24 shorter events, 0.2 us)
Async XLA Ops:
  7.2 116.3 %copy-start = (bf16[4,1,6,128,128]{4,3,2,1,0:T(8,128)(2,1)S(1)}, bf16[4,1,6,128,128]{4,3,2,1,0:T(8,128)(2,1)}, u32[]{:S(2)}) copy-start(bf16[4,1,6,128,128]{4,3,2,1,0:T(8,128)(2,1)} %param.5) | copy-start | bytes 2359300
  7.2 26.2 %copy-start.4 = (f32[1,6,128]{2,0,1:T(1,128)S(1)}, f32[1,6,128]{2,0,1:T(1,128)}, u32[]{:S(2)}) copy-start(f32[1,6,128]{2,0,1:T(1,128)} %param.7) | copy-start | bytes 9220
  7.2 151.2 %all-gather.7.cloned.1.call-start = ((), (), s32[]{:S(2)}) async-start(), calls=%async_computation.3 | async-start | bytes 3538944 | tf_op jit(solution)/shard_map/all_gather | solution.py:336
  9.2 115.2 %copy-start.2 = (f32[1,6,32,128]{3,2,1,0:T(8,128)S(1)}, f32[1,6,32,128]{3,2,1,0:T(8,128)}, u32[]{:S(2)}) copy-start(f32[1,6,32,128]{3,2,1,0:T(8,128)} %param.4) | copy-start | bytes 294916
  9.4 17.5 %collective-permute-start = (bf16[3,1,6,128,128]{4,3,2,0,1:T(8,128)(2,1)S(1)}, bf16[3,1,6,128,128]{4,3,2,0,1:T(8,128)(2,1)S(1)}, u32[]{:S(2)}, u32[]{:S(2)}) collective-permute-start(bf16[3,1,6,128,128]{4,3,2,0,1:T(8,128)(2,1)S(1)} %pad_maximum_fusion.1), channel_id=1, source_target_pairs={{0,4},{1,5},{2,6},{3,7},{8,12},{9,13},{10,14},{11,15},{16,20},{17,... | collective-permute-start | bytes 1769480 | tf_op jit(solution)/shard_map/ppermute | solution.py:312
  26.9 7.1 %collective-permute-start.2 = (bf16[1,1,1,128,128]{4,3,2,0,1:T(8,128)(2,1)S(1)}, bf16[1,1,1,128,128]{4,3,2,0,1:T(8,128)(2,1)S(1)}, u32[]{:S(2)}, u32[]{:S(2)}) collective-permute-start(bf16[1,1,1,128,128]{4,3,2,0,1:T(8,128)(2,1)S(1)} %slice.60), channel_id=1, source_target_pairs={{1,0},{2,1},{3,2},{5,4},{6,5},{7,6},{9,8},{10,9},{11,10},{13,12},{... | collective-permute-start | bytes 98312 | tf_op jit(solution)/shard_map/ppermute | solution.py:315
  28.2 5.8 %collective-permute-start.1 = (bf16[2,1,1,128,128]{4,3,2,0,1:T(8,128)(2,1)S(1)}, bf16[2,1,1,128,128]{4,3,2,0,1:T(8,128)(2,1)S(1)}, u32[]{:S(2)}, u32[]{:S(2)}) collective-permute-start(bf16[2,1,1,128,128]{4,3,2,0,1:T(8,128)(2,1)S(1)} %pad_maximum_fusion.3), channel_id=1, source_target_pairs={{0,1},{1,2},{2,3},{4,5},{5,6},{6,7},{8,9},{9,10},{10,11},{12,13},{... | collective-permute-start | bytes 196616 | tf_op jit(solution)/shard_map/ppermute | solution.py:312
  34.0 96.2 %copy-start.3 = (f32[1,6,128]{2,1,0:T(8,128)S(1)}, f32[1,6,128]{2,1,0:T(8,128)}, u32[]{:S(2)}) copy-start(f32[1,6,128]{2,1,0:T(8,128)} %copy.28) | copy-start | bytes 9220
  123.4 82.3 %all-gather.5.cloned.1.call-start = ((), (), s32[]{:S(2)}) async-start(), calls=%async_computation.2 | async-start | bytes 7077888 | tf_op jit(solution)/shard_map/all_gather | solution.py:324
  125.1 15.9 %all-to-all-start = ((f32[8,6,4,128]{3,2,1,0:T(4,128)}), f32[8,6,4,128]{3,2,1,0:T(4,128)S(1)}, u32[]{:S(2)}, u32[]{:S(2)}) async-start(f32[8,6,4,128]{3,2,1,0:T(4,128)} %bitcast.26), calls=%async_computation | async-start | bytes 196608 | tf_op jit(solution)/shard_map/all_to_all | solution.py:334
  141.0 64.7 %copy-start.1 = (f32[8,6,4,128]{3,2,1,0:T(4,128)}, f32[8,6,4,128]{3,2,1,0:T(4,128)S(1)}, u32[]{:S(2)}) copy-start(f32[8,6,4,128]{3,2,1,0:T(4,128)S(1)} %all-to-all-done.load) | copy-start | bytes 294916
Sparse Core Ops, SparseCore 0:
  123.5 34.8 all-gather.6
  160.2 45.3 all-gather.4

commit v2 on v1

--- a/solution.py
+++ b/solution.py
@@ -134,7 +134,7 @@
     return first, second, third
 
 
-def invert_kernel(ahead, behind, shift, out, work):
+def invert_kernel(ahead, behind, shift, out, *work):
     nodes = shift.shape[0]
     rows = lax.broadcasted_iota(jnp.int32, (B, B), 0)
     lanes = lax.broadcasted_iota(jnp.int32, (B, B), 1)
@@ -143,23 +143,28 @@
         for d in range(len(OFFSETS)):
             total = total + gram(ahead[d, node])
             total = total + gram(behind[d, node])
-        work[node] = total
+        work[node][...] = total
 
     def step(k, carry):
-        lane = lax.broadcasted_iota(jnp.int32, (1, B), 1)
-        for node in range(nodes):
-            block = work[node]
-            row = work[node, pl.ds(k, 1), :]
-            column = jnp.take_along_axis(block, jnp.full((B, B), k, jnp.int32), axis=1)
-            pivot = jnp.sum(jnp.where(lane == k, row, 0.0), axis=1, keepdims=True)
-            scaled = jnp.where(lane == k, 1.0, row) / pivot
-            work[node] = jnp.where(lanes == k, 0.0, block) - column * scaled
-            work[node, pl.ds(k, 1), :] = scaled
+        lane = lax.broadcasted_iota(jnp.int32, (nodes, B), 1)
+        picked = jnp.concatenate([block[pl.ds(k, 1), :] for block in work], axis=0)
+        pivot = jnp.sum(jnp.where(lane == k, picked, 0.0), axis=1, keepdims=True)
+        scaled = jnp.where(lane == k, 1.0, picked) / pivot
+        index = jnp.full((8, B), k, jnp.int32)
+        other = lane[:1] == k
+        for node, block in enumerate(work):
+            row = scaled[node : node + 1]
+            for top in range(0, B, 8):
+                part = block[top : top + 8]
+                column = jnp.take_along_axis(part, index, axis=1)
+                block[top : top + 8] = jnp.where(other, 0.0, part) - column * row
+        for node, block in enumerate(work):
+            block[pl.ds(k, 1), :] = scaled[node : node + 1]
         return carry
 
     lax.fori_loop(0, B, step, 0)
     for node in range(nodes):
-        out[node] = work[node]
+        out[node] = work[node][...]
 
 
 def invert(ahead, behind, shift):
@@ -169,8 +174,26 @@
         out_shape=jax.ShapeDtypeStruct((nodes, B, B), jnp.float32),
         in_specs=[VMEM] * 3,
         out_specs=VMEM,
-        scratch_shapes=[pltpu.VMEM((nodes, B, B), jnp.float32)],
+        scratch_shapes=[pltpu.VMEM((B, B), jnp.float32)] * nodes,
     )(ahead, behind, shift)
+
+
+def spring_kernel(factors, out):
+    for node in range(factors.shape[2]):
+        first, second, _ = split(gram(factors[0, 0, node]))
+        out[0, 0, node, :, :B] = first
+        out[0, 0, node, :, B:] = second
+
+
+def springs_of(factors):
+    devices, directions, nodes = factors.shape[:3]
+    return pl.pallas_call(
+        spring_kernel,
+        grid=(devices, directions),
+        out_shape=jax.ShapeDtypeStruct((devices, directions, nodes, B, 2 * B), jnp.bfloat16),
+        in_specs=[pl.BlockSpec((1, 1, nodes, B, B), lambda i, d: (i, d, 0, 0, 0))],
+        out_specs=pl.BlockSpec((1, 1, nodes, B, 2 * B), lambda i, d: (i, d, 0, 0, 0)),
+    )(factors)
 
 
 def stacked(value):
@@ -191,18 +214,17 @@
 def solve_kernel(nx, ny, nbx, nby):
     ncy = ny // nby
     devices = (nx // nbx) * ncy
-    unroll = 2 if ny % 2 == 0 else 1
-
-    def kernel(load, shift, factors, inverse, out_x, out_r, w, m, p, q, image, x, r, z, mass):
+    unroll = 4 if ny % 4 == 0 else 1
+
+    def kernel(load, shift, springs, inverse, out_x, out_r, w, m, p, q, image, x, r, z, mass, sem):
+        pull = pltpu.make_async_copy(springs, w, sem)
+        pull.start()
+
         def prepare(dev, carry):
             for lx in range(nbx):
                 for ly in range(nby):
                     gx, gy = (dev // ncy) * nbx + lx, (dev % ncy) * nby + ly
                     node = lx * nby + ly
-                    for d in range(len(OFFSETS)):
-                        first, second, _ = split(gram(factors[dev, d, node]))
-                        w[d, gx, gy, :, :B] = first
-                        w[d, gx, gy, :, B:] = second
                     for part, term in enumerate(split(inverse[dev, node])):
                         m[gx, gy, :, part * B : (part + 1) * B] = term
                     field = load[dev, node]
@@ -228,7 +250,7 @@
                     acc = acc + value * precon
                 return acc
 
-            rz = total(lax.fori_loop(0, ny, precondition, zero, unroll=2 * unroll))
+            rz = total(lax.fori_loop(0, ny, precondition, zero, unroll=unroll))
             ratio = rz / rz_old
 
             def advance(y, carry):
@@ -236,16 +258,18 @@
                     p[1 + i, 1 + y] = z[i, y] + ratio * p[1 + i, 1 + y]
                 return carry
 
-            lax.fori_loop(0, ny, advance, 0, unroll=2 * unroll)
-
-            def edges(y, carry):
-                for i in range(nx):
+            lax.fori_loop(0, ny, advance, 0, unroll=unroll)
+
+            def edges(dev, carry):
+                for node in range(nbx * nby):
+                    x_at = 1 + (dev // ncy) * nbx + node // nby
+                    y_at = 1 + (dev % ncy) * nby + node % nby
                     for d, (step_x, step_y) in enumerate(OFFSETS):
-                        delta = p[1 + i, 1 + y] - p[1 + i + step_x, 1 + y + step_y]
-                        q[d, 1 + i, 1 + y] = product(stacked(delta), w[d, i, y])
+                        delta = p[x_at, y_at] - p[x_at + step_x, y_at + step_y]
+                        q[d, x_at, y_at] = product(stacked(delta), w[dev, d, node])
                 return carry
 
-            lax.fori_loop(0, ny, edges, 0, unroll=unroll)
+            lax.fori_loop(0, devices, edges, 0)
 
             def gather(y, acc):
                 for i in range(nx):
@@ -259,7 +283,7 @@
                     acc = acc + value * result
                 return acc
 
-            alpha = rz / total(lax.fori_loop(0, ny, gather, zero, unroll=2 * unroll))
+            alpha = rz / total(lax.fori_loop(0, ny, gather, zero, unroll=unroll))
 
             def update(y, carry):
                 for i in range(nx):
@@ -267,9 +291,10 @@
                     r[i, y] = r[i, y] - alpha * image[i, y]
                 return carry
 
-            lax.fori_loop(0, ny, update, 0, unroll=2 * unroll)
+            lax.fori_loop(0, ny, update, 0, unroll=unroll)
             return rz
 
+        pull.wait()
         lax.fori_loop(0, ITERS, iterate, jnp.ones((2 * ROWS, 1), jnp.float32))
 
         def finish(dev, carry):
@@ -285,23 +310,24 @@
     return kernel
 
 
-def solve(load, shift, factors, inverse, nx, ny, nbx, nby):
+def solve(load, shift, springs, inverse, nx, ny, nbx, nby):
     tall = 2 * ROWS
     field = pltpu.VMEM((nx, ny, tall, B), jnp.float32)
     return pl.pallas_call(
         solve_kernel(nx, ny, nbx, nby),
         out_shape=[jax.ShapeDtypeStruct(load.shape, jnp.float32)] * 2,
-        in_specs=[VMEM] * 4,
+        in_specs=[VMEM, VMEM, pl.BlockSpec(memory_space=pl.ANY), VMEM],
         out_specs=[VMEM] * 2,
         scratch_shapes=[
-            pltpu.VMEM((len(OFFSETS), nx, ny, B, 2 * B), jnp.bfloat16),
+            pltpu.VMEM(springs.shape, jnp.bfloat16),
             pltpu.VMEM((nx, ny, B, 3 * B), jnp.bfloat16),
             pltpu.VMEM((nx + 2, ny + 2, tall, B), jnp.float32),
             pltpu.VMEM((len(OFFSETS), nx + 2, ny + 2, tall, B), jnp.float32),
         ]
-        + [field] * 5,
+        + [field] * 5
+        + [pltpu.SemaphoreType.DMA(())],
         compiler_params=pltpu.CompilerParams(vmem_limit_bytes=VMEM_BYTES),
-    )(load, shift, factors, inverse)
+    )(load, shift, springs, inverse)
 
 
 def shifted(cells, axis, dim, step):
@@ -333,8 +359,10 @@
     columns = load.reshape(nodes, devices, ROWS, B).transpose(1, 0, 2, 3)
     columns = lax.all_to_all(columns, GRID_AXES, 0, 0)
     shifts = lax.all_gather(flat_shift, GRID_AXES)
+    gathered, inverse = lax.optimization_barrier((gathered, inverse))
     inverses = lax.all_gather(inverse, GRID_AXES)
-    outs = solve(columns, shifts, gathered, inverses, gx * nbx, gy * nby, nbx, nby)
+    springs = springs_of(gathered)
+    outs = solve(columns, shifts, springs, inverses, gx * nbx, gy * nby, nbx, nby)
     outs = lax.all_to_all(jnp.stack(outs, axis=1), GRID_AXES, 0, 0)
     outs = outs.transpose(1, 2, 0, 3, 4).reshape(2, nbx, nby, rhs, B)
     return (outs[0], outs[1])

time: 275 us -> 178 us (0.65)
  waiting for transfers between devices: 77.2 us -> 22.8 us
  Pallas kernels: 140 us -> 95.9 us
    pallas_call x1, Pallas kernels: 88.3 us -> 29 us  [invert(): pl.pallas_call(invert_kernel, out_shape=jax.ShapeDtypeStruct((nodes, B, B...]
    all_gather x1, waiting for transfers between devices: 47.3 us -> 0.01 us  [local_columns(): gathered = lax.all_gather(masked.reshape(4, nodes, B, B), GRID_AXES)]
    pallas_call x0 -> x1, Pallas kernels: none -> 23.2 us  [springs_of(): pl.pallas_call(spring_kernel, grid=(devices, directions), out_shape=jax.S...]
    all_gather x1, waiting for transfers between devices: 17.4 us -> 0.01 us  [local_columns(): inverses = lax.all_gather(inverse, GRID_AXES)]
    ppermute x2, waiting for transfers between devices: 12.5 us -> 21 us  [shifted(): rim = lax.ppermute(rim, axis, [(i, i + 1) for i in range(count - 1)])]
    pallas_call x1, Pallas kernels: 51.3 us -> 43.7 us  [solve(): pl.pallas_call(solve_kernel(nx, ny, nbx, nby), out_shape=[jax.ShapeDtypeS...]
  transfers between devices with their start and end apart: 6 -> 6, of which waited for: 3 -> 2; matrix products, arithmetic and copies ran while one was open for 2% -> 3% of each run, Pallas kernels for 0% -> 29%
where the time goes in v2:
time: 178 us; the launch traced here: 177 us
  Pallas kernels  95.9 us (54%)
  waiting for transfers between devices  22.8 us (13%)
  blocking collectives  20 us (11%)
  between operations  14.2 us (8%)
  starting transfers between devices  13.9 us (8%)
  other arithmetic  7.22 us (4%)
  local copies, waits for them, and re-layouts  3.33 us (2%)
    pallas_call x1, Pallas kernels, solve(): pl.pallas_call(solve_kernel(nx, ny, nbx, nby), out_shape=[jax.ShapeDtypeS...  43.7 us
    pallas_call x1, Pallas kernels, invert(): pl.pallas_call(invert_kernel, out_shape=jax.ShapeDtypeStruct((nodes, B, B...  29 us
    pallas_call x1, Pallas kernels, springs_of(): pl.pallas_call(spring_kernel, grid=(devices, directions), out_shape=jax.S...  23.2 us
    ppermute x2, waiting for transfers between devices, shifted(): rim = lax.ppermute(rim, axis, [(i, i + 1) for i in range(count - 1)])  21 us
    all_gather x1, blocking collectives, local_columns(): shifts = lax.all_gather(flat_shift, GRID_AXES)  11.4 us
    all_to_all x1, blocking collectives, local_columns(): outs = lax.all_to_all(jnp.stack(outs, axis=1), GRID_AXES, 0, 0)  8.6 us
    all_to_all x1, starting transfers between devices, local_columns(): columns = lax.all_to_all(columns, GRID_AXES, 0, 0)  6.25 us
    ppermute x2, starting transfers between devices, shifted(): rim = lax.ppermute(rim, axis, [(i, i + 1) for i in range(count - 1)])  6.23 us
  transfers between devices with their start and end apart: 6, of which 2 were waited for; matrix products, arithmetic and copies ran while one was open for 3% of the time, Pallas kernels for 29%

profile of v2, /device:TPU:0, one launch (start us, length us, event | category | flops | bytes accessed | tf_op | source)
XLA Modules:
  0.0 177.4 jit_solution(6915974664347799640)
XLA Ops:
  7.2 0.7 convert_element_type.3
  8.0 2.1 %fusion.8 = bf16[4,1,6,128,128]{4,3,2,1,0:T(8,128)(2,1)} fusion(bf16[4,6]{1,0:T(4,128)(2,1)S(1)} %bitcast.38, bf16[4,1,6,128,128]{4,3,2,1,0:T(8,128)(2,1)} %param.5), kind=kLoop, calls=%fused_computation.16 | loop fusion | flops 393216 | bytes 1572912 | tf_op jit(solution)/shard_map/mul | solution.py:349
  10.2 0.0 all-gather.7.cloned.1.call-start
  10.2 1.3 bitcast_multiply_fusion
  11.5 0.1 pad_maximum_fusion.1
  11.6 4.9 %collective-permute-start = (bf16[3,1,6,128,128]{4,3,2,0,1:T(8,128)(2,1)S(1)}, bf16[3,1,6,128,128]{4,3,2,0,1:T(8,128)(2,1)S(1)}, u32[]{:S(2)}, u32[]{:S(2)}) collective-permute-start(bf16[3,1,6,128,128]{4,3,2,0,1:T(8,128)(2,1)S(1)} %pad_maximum_fusion.1), channel_id=1, source_target_pairs={{0,4},{1,5},{2,6},{3,7},{8,12},{9,13},{10,14},{11,15},{16,20},{17,... | collective-permute-start | bytes 1769480 | tf_op jit(solution)/shard_map/ppermute | solution.py:338
  16.5 21.0 %collective-permute-done = bf16[3,1,6,128,128]{4,3,2,0,1:T(8,128)(2,1)S(1)} collective-permute-done((bf16[3,1,6,128,128]{4,3,2,0,1:T(8,128)(2,1)S(1)}, bf16[3,1,6,128,128]{4,3,2,0,1:T(8,128)(2,1)S(1)}, u32[]{:S(2)}, u32[]{:S(2)}) %collective-permute-start) | collective-permute-done | bytes 589856 | tf_op jit(solution)/shard_map/ppermute | solution.py:338
  37.6 1.3 collective-permute-start.1
  38.9 1.3 collective-permute-start.2
  40.2 1.0 fusion.7.ahead
  41.2 0.6 copy.28
  41.8 1.8 %collective-permute-done.2 = bf16[1,1,1,128,128]{4,3,2,0,1:T(8,128)(2,1)S(1)} collective-permute-done((bf16[1,1,1,128,128]{4,3,2,0,1:T(8,128)(2,1)S(1)}, bf16[1,1,1,128,128]{4,3,2,0,1:T(8,128)(2,1)S(1)}, u32[]{:S(2)}, u32[]{:S(2)}) %collective-permute-start.2) | collective-permute-done | bytes 32800 | tf_op jit(solution)/shard_map/ppermute | solution.py:341
  43.6 1.0 fusion.3.behind
  44.6 29.0 %shard_map.59 = f32[6,128,128]{2,1,0:T(8,128)} custom-call(bf16[4,6,128,128]{3,2,1,0:T(8,128)(2,1)} %fusion.7.ahead, bf16[4,6,128,128]{3,2,1,0:T(8,128)(2,1)} %fusion.3.behind, f32[6,128]{1,0:T(8,128)} %bitcast.37), custom_call_target="tpu_custom_call" | custom-call | tf_op jit(solution)/shard_map/pallas_call | solution.py:172
  73.7 0.7 copy.26
  74.3 6.3 %all-to-all-start = ((f32[8,6,4,128]{3,2,1,0:T(4,128)}), f32[8,6,4,128]{3,2,1,0:T(4,128)S(1)}, u32[]{:S(2)}, u32[]{:S(2)}) async-start(f32[8,6,4,128]{3,2,1,0:T(4,128)} %bitcast.26), calls=%async_computation | async-start | bytes 196608 | tf_op jit(solution)/shard_map/all_to_all | solution.py:360
  80.6 11.4 %all_gather.12.shift = f32[8,6,128]{2,1,0:T(8,128)} all-gather(f32[1,6,128]{2,1,0:T(8,128)} %copy.28), channel_id=1, replica_groups=mesh['case'=4,'gx'=2,'gy'=4] {'gx','gy'}, dimensions={0}, use_global_device_ids=true | all-gather | bytes 27648 | tf_op jit(solution)/shard_map/all_gather | solution.py:361
  92.0 23.2 %shard_map.60.springs = bf16[8,4,6,128,256]{4,3,2,1,0:T(8,128)(2,1)} custom-call(bf16[8,4,6,128,128]{4,3,2,1,0:T(8,128)(2,1)} %bitcast.29), custom_call_target="tpu_custom_call" | custom-call | tf_op jit(solution)/shard_map/pallas_call | solution.py:190
  115.2 0.6 copy-done.1
  115.8 43.7 %shard_map.61 = (f32[8,6,4,128]{3,2,1,0:T(4,128)}, f32[8,6,4,128]{3,2,1,0:T(4,128)}) custom-call(f32[8,6,4,128]{3,2,1,0:T(4,128)} %copy-done.1, f32[8,6,128]{2,1,0:T(8,128)} %all_gather.12.shift, bf16[8,4,6,128,256]{4,3,2,1,0:T(8,128)(2,1)} %shard_map.60.springs, f32[8,6,128,128]{3,2,1,0:T(8,128)} %bitcast.30), custom_call_target="tpu_custom_call" | custom-call | tf_op jit(solution)/shard_map/pallas_call | solution.py:316
  159.6 1.0 pad_maximum_fusion.2
  160.6 8.6 %all_to_all.10 = f32[8,2,6,4,128]{4,3,2,1,0:T(4,128)S(1)} all-to-all(f32[8,2,6,4,128]{4,3,2,1,0:T(4,128)S(1)} %copy.17), channel_id=1, replica_groups=mesh['case'=4,'gx'=2,'gy'=4] {'gx','gy'}, dimensions={0} | all-to-all | bytes 393216 | tf_op jit(solution)/shard_map/all_to_all | solution.py:366
  169.2 0.7 copy.18
  169.9 0.7 copy.19
  (23 shorter events, 0.2 us)
Async XLA Ops:
  7.2 33.0 %copy-start = (bf16[4,1,6,128,128]{4,3,2,1,0:T(8,128)(2,1)S(1)}, bf16[4,1,6,128,128]{4,3,2,1,0:T(8,128)(2,1)}, u32[]{:S(2)}) copy-start(bf16[4,1,6,128,128]{4,3,2,1,0:T(8,128)(2,1)} %param.5) | copy-start | bytes 2359300
  7.2 34.0 %copy-start.3 = (f32[1,6,128]{2,0,1:T(1,128)S(1)}, f32[1,6,128]{2,0,1:T(1,128)}, u32[]{:S(2)}) copy-start(f32[1,6,128]{2,0,1:T(1,128)} %param.7) | copy-start | bytes 9220
  7.2 66.5 %all-gather.5.cloned.1.call-start = ((), (), s32[]{:S(2)}) async-start(), calls=%async_computation.2 | async-start | bytes 7077888 | tf_op jit(solution)/shard_map/all_gather | solution.py:350
  10.1 63.5 %copy-start.2 = (f32[1,6,32,128]{3,2,1,0:T(8,128)S(1)}, f32[1,6,32,128]{3,2,1,0:T(8,128)}, u32[]{:S(2)}) copy-start(f32[1,6,32,128]{3,2,1,0:T(8,128)} %param.4) | copy-start | bytes 294916
  10.2 105.1 %all-gather.7.cloned.1.call-start = ((), (), s32[]{:S(2)}) async-start(), calls=%async_computation.3 | async-start | bytes 3538944 | tf_op jit(solution)/shard_map/all_gather | solution.py:363
  11.6 25.9 %collective-permute-start = (bf16[3,1,6,128,128]{4,3,2,0,1:T(8,128)(2,1)S(1)}, bf16[3,1,6,128,128]{4,3,2,0,1:T(8,128)(2,1)S(1)}, u32[]{:S(2)}, u32[]{:S(2)}) collective-permute-start(bf16[3,1,6,128,128]{4,3,2,0,1:T(8,128)(2,1)S(1)} %pad_maximum_fusion.1), channel_id=1, source_target_pairs={{0,4},{1,5},{2,6},{3,7},{8,12},{9,13},{10,14},{11,15},{16,20},{17,... | collective-permute-start | bytes 1769480 | tf_op jit(solution)/shard_map/ppermute | solution.py:338
  37.6 6.1 %collective-permute-start.1 = (bf16[2,1,1,128,128]{4,3,2,0,1:T(8,128)(2,1)S(1)}, bf16[2,1,1,128,128]{4,3,2,0,1:T(8,128)(2,1)S(1)}, u32[]{:S(2)}, u32[]{:S(2)}) collective-permute-start(bf16[2,1,1,128,128]{4,3,2,0,1:T(8,128)(2,1)S(1)} %pad_maximum_fusion.3), channel_id=1, source_target_pairs={{0,1},{1,2},{2,3},{4,5},{5,6},{6,7},{8,9},{9,10},{10,11},{12,13},{... | collective-permute-start | bytes 196616 | tf_op jit(solution)/shard_map/ppermute | solution.py:338
  38.9 4.8 %collective-permute-start.2 = (bf16[1,1,1,128,128]{4,3,2,0,1:T(8,128)(2,1)S(1)}, bf16[1,1,1,128,128]{4,3,2,0,1:T(8,128)(2,1)S(1)}, u32[]{:S(2)}, u32[]{:S(2)}) collective-permute-start(bf16[1,1,1,128,128]{4,3,2,0,1:T(8,128)(2,1)S(1)} %slice.60), channel_id=1, source_target_pairs={{1,0},{2,1},{3,2},{5,4},{6,5},{7,6},{9,8},{10,9},{11,10},{13,12},{... | collective-permute-start | bytes 98312 | tf_op jit(solution)/shard_map/ppermute | solution.py:341
  74.3 40.9 %all-to-all-start = ((f32[8,6,4,128]{3,2,1,0:T(4,128)}), f32[8,6,4,128]{3,2,1,0:T(4,128)S(1)}, u32[]{:S(2)}, u32[]{:S(2)}) async-start(f32[8,6,4,128]{3,2,1,0:T(4,128)} %bitcast.26), calls=%async_computation | async-start | bytes 196608 | tf_op jit(solution)/shard_map/all_to_all | solution.py:360
  115.2 0.6 copy-start.1
Sparse Core Ops, SparseCore 0:
  10.3 55.5 all-gather.4
  73.8 36.2 all-gather.6

commit v3 on v2

--- a/solution.py
+++ b/solution.py
@@ -163,37 +163,61 @@
         return carry
 
     lax.fori_loop(0, B, step, 0)
-    for node in range(nodes):
-        out[node] = work[node][...]
+    pairs = (nodes + 1) // 2
+    out[pairs * B :] = jnp.zeros((out.shape[0] - pairs * B, B), jnp.float32)
+    for pair in range(pairs):
+        lower = work[2 * pair][...]
+        upper = work[min(2 * pair + 1, nodes - 1)][...]
+        lower = 0.5 * (lower + lower.T)
+        upper = 0.5 * (upper + upper.T)
+        out[pair * B : (pair + 1) * B] = jnp.where(rows >= lanes, lower, upper)
+        diagonal = jnp.sum(jnp.where(rows == lanes, upper, 0.0), axis=0, keepdims=True)
+        out[pairs * B + pair : pairs * B + pair + 1] = diagonal
+
+
+def unpacked(packed, diagonal):
+    rows = lax.broadcasted_iota(jnp.int32, (B, B), 0)
+    lanes = lax.broadcasted_iota(jnp.int32, (B, B), 1)
+    turned = packed.T
+    lower = jnp.where(rows >= lanes, packed, turned)
+    upper = jnp.where(rows < lanes, packed, turned)
+    return lower, jnp.where(rows == lanes, diagonal, upper)
 
 
 def invert(ahead, behind, shift):
     nodes = shift.shape[0]
+    pairs = (nodes + 1) // 2
     return pl.pallas_call(
         invert_kernel,
-        out_shape=jax.ShapeDtypeStruct((nodes, B, B), jnp.float32),
+        out_shape=jax.ShapeDtypeStruct((pairs * B + (pairs + 7) // 8 * 8, B), jnp.float32),
         in_specs=[VMEM] * 3,
         out_specs=VMEM,
         scratch_shapes=[pltpu.VMEM((B, B), jnp.float32)] * nodes,
     )(ahead, behind, shift)
 
 
-def spring_kernel(factors, out):
-    for node in range(factors.shape[2]):
-        first, second, _ = split(gram(factors[0, 0, node]))
-        out[0, 0, node, :, :B] = first
-        out[0, 0, node, :, B:] = second
-
-
-def springs_of(factors):
+def spring_kernel(factors, small, out):
+    _, directions, nodes = factors.shape[:3]
+    for node in range(nodes):
+        for d in range(directions):
+            link = small[0, node : node + 1, B + d : B + d + 1]
+            first, second, _ = split(gram(factors[0, d, node]) * link)
+            out[0, d, node, :, :B] = first
+            out[0, d, node, :, B:] = second
+
+
+def springs_of(factors, small):
     devices, directions, nodes = factors.shape[:3]
     return pl.pallas_call(
         spring_kernel,
-        grid=(devices, directions),
+        grid=(devices,),
         out_shape=jax.ShapeDtypeStruct((devices, directions, nodes, B, 2 * B), jnp.bfloat16),
-        in_specs=[pl.BlockSpec((1, 1, nodes, B, B), lambda i, d: (i, d, 0, 0, 0))],
-        out_specs=pl.BlockSpec((1, 1, nodes, B, 2 * B), lambda i, d: (i, d, 0, 0, 0)),
-    )(factors)
+        in_specs=[
+            pl.BlockSpec((1, directions, nodes, B, B), lambda i: (i, 0, 0, 0, 0)),
+            pl.BlockSpec((1, nodes, 2 * B), lambda i: (i, 0, 0)),
+        ],
+        out_specs=pl.BlockSpec((1, directions, nodes, B, 2 * B), lambda i: (i, 0, 0, 0, 0)),
+    )(factors, small)
 
 
 def stacked(value):
@@ -214,9 +238,10 @@
 def solve_kernel(nx, ny, nbx, nby):
     ncy = ny // nby
     devices = (nx // nbx) * ncy
-    unroll = 4 if ny % 4 == 0 else 1
-
-    def kernel(load, shift, springs, inverse, out_x, out_r, w, m, p, q, image, x, r, z, mass, sem):
+    pairs = (nbx * nby + 1) // 2
+    unroll = next(step for step in (8, 6, 4, 3, 2, 1) if ny % step == 0)
+
+    def kernel(load, small, springs, inverse, out, w, m, p, q, image, x, r, z, mass, sem):
         pull = pltpu.make_async_copy(springs, w, sem)
         pull.start()
 
@@ -225,26 +250,37 @@
                 for ly in range(nby):
                     gx, gy = (dev // ncy) * nbx + lx, (dev % ncy) * nby + ly
                     node = lx * nby + ly
-                    for part, term in enumerate(split(inverse[dev, node])):
+                    if node % 2 == 0:
+                        at = pairs * B + node // 2
+                        blocks = unpacked(
+                            inverse[dev, node // 2 * B : (node // 2 + 1) * B],
+                            inverse[dev, at : at + 1],
+                        )
+                    for part, term in enumerate(split(blocks[node % 2])):
                         m[gx, gy, :, part * B : (part + 1) * B] = term
                     field = load[dev, node]
                     r[gx, gy] = jnp.concatenate([field, field], axis=0)
-                    mass[gx, gy] = jnp.broadcast_to(shift[dev, pl.ds(node, 1), :], (2 * ROWS, B))
+                    mass[gx, gy] = jnp.broadcast_to(small[dev, node : node + 1, :B], (2 * ROWS, B))
             return carry
 
         lax.fori_loop(0, devices, prepare, 0)
         p[...] = jnp.zeros_like(p)
         q[...] = jnp.zeros_like(q)
         x[...] = jnp.zeros_like(x)
+        image[...] = jnp.zeros_like(image)
         zero = jnp.zeros((2 * ROWS, B), jnp.float32)
 
         def total(values):
             return jnp.sum(values, axis=1, keepdims=True)
 
-        def iterate(_, rz_old):
+        def iterate(_, carried):
+            rz_old, alpha = carried
+
             def precondition(y, acc):
                 for i in range(nx):
-                    value = r[i, y]
+                    value = r[i, y] - alpha * image[i, y]
+                    r[i, y] = value
+                    x[i, y] = x[i, y] + alpha * p[1 + i, 1 + y]
                     precon = product(stacked(value), m[i, y])
                     z[i, y] = precon
                     acc = acc + value * precon
@@ -285,24 +321,18 @@
 
             alpha = rz / total(lax.fori_loop(0, ny, gather, zero, unroll=unroll))
 
-            def update(y, carry):
-                for i in range(nx):
-                    x[i, y] = x[i, y] + alpha * p[1 + i, 1 + y]
-                    r[i, y] = r[i, y] - alpha * image[i, y]
-                return carry
-
-            lax.fori_loop(0, ny, update, 0, unroll=unroll)
-            return rz
+            return rz, alpha
 
         pull.wait()
-        lax.fori_loop(0, ITERS, iterate, jnp.ones((2 * ROWS, 1), jnp.float32))
+        one = jnp.ones((2 * ROWS, 1), jnp.float32)
+        _, alpha = lax.fori_loop(0, ITERS, iterate, (one, jnp.zeros_like(one)))
 
         def finish(dev, carry):
             for lx in range(nbx):
                 for ly in range(nby):
                     gx, gy = (dev // ncy) * nbx + lx, (dev % ncy) * nby + ly
-                    out_x[dev, lx * nby + ly] = x[gx, gy][:ROWS]
-                    out_r[dev, lx * nby + ly] = r[gx, gy][:ROWS]
+                    out[dev, 0, lx * nby + ly] = (x[gx, gy] + alpha * p[1 + gx, 1 + gy])[:ROWS]
+                    out[dev, 1, lx * nby + ly] = (r[gx, gy] - alpha * image[gx, gy])[:ROWS]
             return carry
 
         lax.fori_loop(0, devices, finish, 0)
@@ -310,14 +340,14 @@
     return kernel
 
 
-def solve(load, shift, springs, inverse, nx, ny, nbx, nby):
+def solve(load, small, springs, inverse, nx, ny, nbx, nby):
     tall = 2 * ROWS
     field = pltpu.VMEM((nx, ny, tall, B), jnp.float32)
     return pl.pallas_call(
         solve_kernel(nx, ny, nbx, nby),
-        out_shape=[jax.ShapeDtypeStruct(load.shape, jnp.float32)] * 2,
+        out_shape=jax.ShapeDtypeStruct((load.shape[0], 2) + load.shape[1:], jnp.float32),
         in_specs=[VMEM, VMEM, pl.BlockSpec(memory_space=pl.ANY), VMEM],
-        out_specs=[VMEM] * 2,
+        out_specs=VMEM,
         scratch_shapes=[
             pltpu.VMEM(springs.shape, jnp.bfloat16),
             pltpu.VMEM((nx, ny, B, 3 * B), jnp.bfloat16),
@@ -327,7 +357,7 @@
         + [field] * 5
         + [pltpu.SemaphoreType.DMA(())],
         compiler_params=pltpu.CompilerParams(vmem_limit_bytes=VMEM_BYTES),
-    )(load, shift, springs, inverse)
+    )(load, small, springs, inverse)
 
 
 def shifted(cells, axis, dim, step):
@@ -346,24 +376,27 @@
     nbx, nby, rhs, _ = load.shape
     gx, gy = (lax.axis_size(axis) for axis in GRID_AXES)
     devices, nodes = gx * gy, nbx * nby
+    gathered = lax.all_gather(factors.reshape(4, nodes, B, B), GRID_AXES)
     masked = factors * links.astype(jnp.bfloat16)[:, :, :, None, None]
-    gathered = lax.all_gather(masked.reshape(4, nodes, B, B), GRID_AXES)
     down = shifted(jnp.stack([masked[0], masked[2], masked[3]]), "gx", 1, 1)
+    flat_links = links.reshape(len(OFFSETS), nodes).T.astype(jnp.float32)
+    flat_links = jnp.pad(flat_links, ((0, 0), (0, B - len(OFFSETS))))
+    small = jnp.concatenate([shift.reshape(nodes, B), flat_links], axis=1)
+    small = lax.all_gather(small, GRID_AXES)
+    columns = load.reshape(nodes, devices, ROWS, B).transpose(1, 0, 2, 3)
+    columns = lax.all_to_all(columns, GRID_AXES, 0, 0)
+    down, small, columns = lax.optimization_barrier((down, small, columns))
     left = shifted(jnp.stack([masked[1], down[1]]), "gy", 2, 1)
     right = shifted(down[2:], "gy", 2, -1)
     behind = jnp.stack([down[0], left[0], left[1], right[0]])
-    flat_shift = shift.reshape(nodes, B)
     inverse = invert(
-        masked.reshape(4, nodes, B, B), behind.reshape(4, nodes, B, B), flat_shift
-    )
-    columns = load.reshape(nodes, devices, ROWS, B).transpose(1, 0, 2, 3)
-    columns = lax.all_to_all(columns, GRID_AXES, 0, 0)
-    shifts = lax.all_gather(flat_shift, GRID_AXES)
+        masked.reshape(4, nodes, B, B), behind.reshape(4, nodes, B, B), shift.reshape(nodes, B)
+    )
     gathered, inverse = lax.optimization_barrier((gathered, inverse))
     inverses = lax.all_gather(inverse, GRID_AXES)
-    springs = springs_of(gathered)
-    outs = solve(columns, shifts, springs, inverses, gx * nbx, gy * nby, nbx, nby)
-    outs = lax.all_to_all(jnp.stack(outs, axis=1), GRID_AXES, 0, 0)
+    springs = springs_of(gathered, small)
+    outs = solve(columns, small, springs, inverses, gx * nbx, gy * nby, nbx, nby)
+    outs = lax.all_to_all(outs, GRID_AXES, 0, 0)
     outs = outs.transpose(1, 2, 0, 3, 4).reshape(2, nbx, nby, rhs, B)
     return (outs[0], outs[1])
 

time: 178 us -> 167 us (0.938)
  Pallas kernels: 95.9 us -> 79.2 us
  blocking collectives: 20 us -> 31.6 us
  other arithmetic: 7.22 us -> 4.11 us
  waiting for transfers between devices: 22.8 us -> 20.9 us
    ppermute x2, waiting for transfers between devices: 21 us -> 0.01 us  [shifted(): rim = lax.ppermute(rim, axis, [(i, i + 1) for i in range(count - 1)])]
    all_gather x1, waiting for transfers between devices: 0.01 us -> 20.2 us  [local_columns(): inverses = lax.all_gather(inverse, GRID_AXES)]
    pallas_call x3, Pallas kernels: 95.9 us -> 79.2 us  [the longest x1 39.4 us: solve(): pl.pallas_call(solve_kernel(nx, ny, nbx, nby), out_shape=jax.ShapeDtypeSt...]
    all_gather x1, blocking collectives: 11.4 us -> 22.1 us  [local_columns(): small = lax.all_gather(small, GRID_AXES)]
    all_to_all x1, starting transfers between devices: 6.25 us -> 3.37 us  [local_columns(): columns = lax.all_to_all(columns, GRID_AXES, 0, 0)]
    mul x2 -> x1, other arithmetic: 3.4 us -> 1.25 us  [local_columns(): masked = factors * links.astype(jnp.bfloat16)[:, :, :, None, None]]
    ppermute x1, waiting for transfers between devices: 1.81 us -> 0.01 us  [shifted(): rim = lax.ppermute(rim, axis, [(i + 1, i) for i in range(count - 1)])]
  transfers between devices with their start and end apart: 6 -> 6, of which waited for: 2 -> 1; matrix products, arithmetic and copies ran while one was open for 3% -> 4% of each run, Pallas kernels for 29% -> 24%
where the time goes in v3:
time: 167 us; the launch traced here: 166 us
  Pallas kernels  79.2 us (47%)
  blocking collectives  31.6 us (19%)
  waiting for transfers between devices  20.9 us (13%)
  between operations  14.2 us (9%)
  starting transfers between devices  12.7 us (8%)
  other arithmetic  4.11 us (2%)
  local copies, waits for them, and re-layouts  3.78 us (2%)
    pallas_call x1, Pallas kernels, solve(): pl.pallas_call(solve_kernel(nx, ny, nbx, nby), out_shape=jax.ShapeDtypeSt...  39.4 us
    pallas_call x1, Pallas kernels, invert(): pl.pallas_call(invert_kernel, out_shape=jax.ShapeDtypeStruct((pairs * B +...  28.6 us
    all_gather x1, blocking collectives, local_columns(): small = lax.all_gather(small, GRID_AXES)  22.1 us
    all_gather x1, waiting for transfers between devices, local_columns(): inverses = lax.all_gather(inverse, GRID_AXES)  20.2 us
    pallas_call x1, Pallas kernels, springs_of(): pl.pallas_call(spring_kernel, grid=(devices,), out_shape=jax.ShapeDtypeSt...  11.1 us
    all_to_all x1, blocking collectives, local_columns(): outs = lax.all_to_all(outs, GRID_AXES, 0, 0)  9.51 us
    ppermute x2, starting transfers between devices, shifted(): rim = lax.ppermute(rim, axis, [(i, i + 1) for i in range(count - 1)])  7.97 us
    all_to_all x1, starting transfers between devices, local_columns(): columns = lax.all_to_all(columns, GRID_AXES, 0, 0)  3.37 us
  transfers between devices with their start and end apart: 6, of which 1 were waited for; matrix products, arithmetic and copies ran while one was open for 4% of the time, Pallas kernels for 24%

profile of v3, /device:TPU:0, one launch (start us, length us, event | category | flops | bytes accessed | tf_op | source)
XLA Modules:
  0.0 166.5 jit_solution(2236200748005351569)
XLA Ops:
  7.2 0.0 all-gather.7.cloned.1.call-start
  7.2 0.7 all-gather.7.cloned.1.call-update
  7.9 0.8 fusion.8
  8.7 1.2 bitcast_multiply_fusion
  10.0 0.1 pad_maximum_fusion.1
  10.1 4.9 %collective-permute-start = (bf16[3,1,6,128,128]{4,3,2,0,1:T(8,128)(2,1)S(1)}, bf16[3,1,6,128,128]{4,3,2,0,1:T(8,128)(2,1)S(1)}, u32[]{:S(2)}, u32[]{:S(2)}) collective-permute-start(bf16[3,1,6,128,128]{4,3,2,0,1:T(8,128)(2,1)S(1)} %pad_maximum_fusion.1), channel_id=1, source_target_pairs={{0,4},{1,5},{2,6},{3,7},{8,12},{9,13},{10,14},{11,15},{16,20},{17,... | collective-permute-start | bytes 1769480 | tf_op jit(solution)/shard_map/ppermute | solution.py:368
  15.0 1.6 copy.23
  16.6 3.4 %all-to-all-start = ((f32[8,6,4,128]{3,2,1,0:T(4,128)}), f32[8,6,4,128]{3,2,1,0:T(4,128)S(1)}, u32[]{:S(2)}, u32[]{:S(2)}) async-start(f32[8,6,4,128]{3,2,1,0:T(4,128)} %bitcast.24), calls=%async_computation | async-start | bytes 196608 | tf_op jit(solution)/shard_map/all_to_all | solution.py:387
  19.9 0.0 all-gather.9.cloned.1.call-start
  20.0 0.1 copy.14
  20.1 0.7 copy.24
  20.8 22.1 %all-gather.3.small = f32[8,6,256]{2,1,0:T(8,128)} all-gather(f32[1,6,256]{2,1,0:T(8,128)S(1)} %fusion.4), channel_id=2, replica_groups=mesh['case'=4,'gx'=2,'gy'=4] {'gx','gy'}, dimensions={0}, use_global_device_ids=true | all-gather | bytes 55296 | tf_op jit(solution)/shard_map/all_gather | solution.py:385
  42.9 1.3 collective-permute-start.2
  44.2 3.0 %collective-permute-start.1 = (bf16[2,1,1,128,128]{4,3,2,0,1:T(8,128)(2,1)S(1)}, bf16[2,1,1,128,128]{4,3,2,0,1:T(8,128)(2,1)S(1)}, u32[]{:S(2)}, u32[]{:S(2)}) collective-permute-start(bf16[2,1,1,128,128]{4,3,2,0,1:T(8,128)(2,1)S(1)} %pad_maximum_fusion.2), channel_id=1, source_target_pairs={{0,1},{1,2},{2,3},{4,5},{5,6},{6,7},{8,9},{9,10},{10,11},{12,13},{... | collective-permute-start | bytes 196616 | tf_op jit(solution)/shard_map/ppermute | solution.py:368
  47.3 1.0 fusion.9.ahead
  48.4 1.0 fusion.3.behind
  49.4 28.6 %shard_map.59 = f32[392,128]{1,0:T(8,128)} custom-call(bf16[4,6,128,128]{3,2,1,0:T(8,128)(2,1)} %fusion.9.ahead, bf16[4,6,128,128]{3,2,1,0:T(8,128)(2,1)} %fusion.3.behind, f32[6,128]{1,0:T(8,128)} %bitcast.34), custom_call_target="tpu_custom_call" | custom-call | tf_op jit(solution)/shard_map/pallas_call | solution.py:190
  78.0 0.0 all-gather.9.cloned.1.call-update
  78.0 11.1 %shard_map.60.springs = bf16[8,4,6,128,256]{4,3,2,1,0:T(8,128)(2,1)} custom-call(bf16[8,4,6,128,128]{4,3,2,1,0:T(8,128)(2,1)} %bitcast.27, f32[8,6,256]{2,1,0:T(8,128)} %all-gather.3.small), custom_call_target="tpu_custom_call" | custom-call | tf_op jit(solution)/shard_map/pallas_call | solution.py:211
  89.1 20.2 %all-gather.9.cloned.1.call-done = f32[3136,128]{1,0:T(8,128)} async-done(((f32[392,128]{1,0:T(8,128)}), f32[3136,128]{1,0:T(8,128)}) %all-gather.9.cloned.1.call-update) | async-done | bytes 1605648 | tf_op jit(solution)/shard_map/all_gather | solution.py:396
  109.4 39.4 %shard_map.61 = f32[8,2,6,4,128]{4,3,2,1,0:T(4,128)} custom-call(f32[8,6,4,128]{3,2,1,0:T(4,128)} %copy-done.1, f32[8,6,256]{2,1,0:T(8,128)} %all-gather.3.small, bf16[8,4,6,128,256]{4,3,2,1,0:T(8,128)(2,1)} %shard_map.60.springs, f32[8,392,128]{2,1,0:T(8,128)} %bitcast.28), custom_call_target="tpu_custom_call" | custom-call | tf_op jit(solution)/shard_map/pallas_call | solution.py:346
  148.8 9.5 %all_to_all.10 = f32[8,2,6,4,128]{4,3,2,1,0:T(4,128)S(1)} all-to-all(f32[8,2,6,4,128]{4,3,2,1,0:T(4,128)} %shard_map.61), channel_id=1, replica_groups=mesh['case'=4,'gx'=2,'gy'=4] {'gx','gy'}, dimensions={0} | all-to-all | bytes 393216 | tf_op jit(solution)/shard_map/all_to_all | solution.py:399
  158.3 0.7 copy.16
  159.0 0.7 copy.17
  (20 shorter events, 0.2 us)
Async XLA Ops:
  7.2 40.1 %copy-start = (bf16[4,1,6,128,128]{4,3,2,1,0:T(8,128)(2,1)S(1)}, bf16[4,1,6,128,128]{4,3,2,1,0:T(8,128)(2,1)}, u32[]{:S(2)}) copy-start(bf16[4,1,6,128,128]{4,3,2,1,0:T(8,128)(2,1)} %param.5) | copy-start | bytes 2359300
  7.2 70.8 %all-gather.7.cloned.1.call-start = ((), (), s32[]{:S(2)}) async-start(), calls=%async_computation.2 | async-start | bytes 7077888 | tf_op jit(solution)/shard_map/all_gather | solution.py:379
  10.1 32.8 %collective-permute-start = (bf16[3,1,6,128,128]{4,3,2,0,1:T(8,128)(2,1)S(1)}, bf16[3,1,6,128,128]{4,3,2,0,1:T(8,128)(2,1)S(1)}, u32[]{:S(2)}, u32[]{:S(2)}) collective-permute-start(bf16[3,1,6,128,128]{4,3,2,0,1:T(8,128)(2,1)S(1)} %pad_maximum_fusion.1), channel_id=1, source_target_pairs={{0,4},{1,5},{2,6},{3,7},{8,12},{9,13},{10,14},{11,15},{16,20},{17,... | collective-permute-start | bytes 1769480 | tf_op jit(solution)/shard_map/ppermute | solution.py:368
  16.6 26.3 %all-to-all-start = ((f32[8,6,4,128]{3,2,1,0:T(4,128)}), f32[8,6,4,128]{3,2,1,0:T(4,128)S(1)}, u32[]{:S(2)}, u32[]{:S(2)}) async-start(f32[8,6,4,128]{3,2,1,0:T(4,128)} %bitcast.24), calls=%async_computation | async-start | bytes 196608 | tf_op jit(solution)/shard_map/all_to_all | solution.py:387
  19.9 89.4 %all-gather.9.cloned.1.call-start = ((), (), s32[]{:S(2)}) async-start(), calls=%async_computation.3 | async-start | bytes 1806336 | tf_op jit(solution)/shard_map/all_gather | solution.py:396
  20.8 28.6 %copy-start.2 = (f32[1,6,128]{2,1,0:T(8,128)}, f32[1,6,128]{2,1,0:T(8,128)S(1)}, u32[]{:S(2)}) copy-start(f32[1,6,128]{2,1,0:T(8,128)S(1)} %copy.24) | copy-start | bytes 9220
  42.9 46.3 %copy-start.1 = (f32[8,6,4,128]{3,2,1,0:T(4,128)}, f32[8,6,4,128]{3,2,1,0:T(4,128)S(1)}, u32[]{:S(2)}) copy-start(f32[8,6,4,128]{3,2,1,0:T(4,128)S(1)} %all-to-all-done.load) | copy-start | bytes 294916
  42.9 5.5 %collective-permute-start.2 = (bf16[1,1,1,128,128]{4,3,2,0,1:T(8,128)(2,1)S(1)}, bf16[1,1,1,128,128]{4,3,2,0,1:T(8,128)(2,1)S(1)}, u32[]{:S(2)}, u32[]{:S(2)}) collective-permute-start(bf16[1,1,1,128,128]{4,3,2,0,1:T(8,128)(2,1)S(1)} %slice.51), channel_id=1, source_target_pairs={{1,0},{2,1},{3,2},{5,4},{6,5},{7,6},{9,8},{10,9},{11,10},{13,12},{... | collective-permute-start | bytes 98312 | tf_op jit(solution)/shard_map/ppermute | solution.py:371
  44.2 4.1 %collective-permute-start.1 = (bf16[2,1,1,128,128]{4,3,2,0,1:T(8,128)(2,1)S(1)}, bf16[2,1,1,128,128]{4,3,2,0,1:T(8,128)(2,1)S(1)}, u32[]{:S(2)}, u32[]{:S(2)}) collective-permute-start(bf16[2,1,1,128,128]{4,3,2,0,1:T(8,128)(2,1)S(1)} %pad_maximum_fusion.2), channel_id=1, source_target_pairs={{0,1},{1,2},{2,3},{4,5},{5,6},{6,7},{8,9},{9,10},{10,11},{12,13},{... | collective-permute-start | bytes 196616 | tf_op jit(solution)/shard_map/ppermute | solution.py:368
Sparse Core Ops, SparseCore 0:
  9.9 55.9 all-gather.6
  78.1 31.2 all-gather.8

commit v4 on v3

--- a/solution.py
+++ b/solution.py
@@ -145,11 +145,20 @@
             total = total + gram(behind[d, node])
         work[node][...] = total
 
-    def step(k, carry):
-        lane = lax.broadcasted_iota(jnp.int32, (nodes, B), 1)
-        picked = jnp.concatenate([block[pl.ds(k, 1), :] for block in work], axis=0)
-        pivot = jnp.sum(jnp.where(lane == k, picked, 0.0), axis=1, keepdims=True)
-        scaled = jnp.where(lane == k, 1.0, picked) / pivot
+    lane = lax.broadcasted_iota(jnp.int32, (nodes, B), 1)
+
+    def picked(k):
+        return jnp.concatenate([block[pl.ds(k, 1), :] for block in work], axis=0)
+
+    def entry(values, k):
+        return jnp.sum(jnp.where(lane == k, values, 0.0), axis=1, keepdims=True)
+
+    def step(k, scaled):
+        coming = picked(jnp.minimum(k + 1, B - 1))
+        factor = entry(coming, k)
+        pivot = entry(coming, k + 1) - factor * entry(scaled, k + 1)
+        coming = jnp.where(lane == k, 0.0, coming) - factor * scaled
+        following = jnp.where(lane == k + 1, 1.0, coming) / pivot
         index = jnp.full((8, B), k, jnp.int32)
         other = lane[:1] == k
         for node, block in enumerate(work):
@@ -160,9 +169,10 @@
                 block[top : top + 8] = jnp.where(other, 0.0, part) - column * row
         for node, block in enumerate(work):
             block[pl.ds(k, 1), :] = scaled[node : node + 1]
-        return carry
-
-    lax.fori_loop(0, B, step, 0)
+        return following
+
+    first = picked(0)
+    lax.fori_loop(0, B, step, jnp.where(lane == 0, 1.0, first) / entry(first, 0))
     pairs = (nodes + 1) // 2
     out[pairs * B :] = jnp.zeros((out.shape[0] - pairs * B, B), jnp.float32)
     for pair in range(pairs):
@@ -239,6 +249,7 @@
     ncy = ny // nby
     devices = (nx // nbx) * ncy
     pairs = (nbx * nby + 1) // 2
+    wide = ny // 2 if ny % 2 == 0 else 1
     unroll = next(step for step in (8, 6, 4, 3, 2, 1) if ny % step == 0)
 
     def kernel(load, small, springs, inverse, out, w, m, p, q, image, x, r, z, mass, sem):
@@ -286,7 +297,7 @@
                     acc = acc + value * precon
                 return acc
 
-            rz = total(lax.fori_loop(0, ny, precondition, zero, unroll=unroll))
+            rz = total(lax.fori_loop(0, ny, precondition, zero, unroll=wide))
             ratio = rz / rz_old
 
             def advance(y, carry):
@@ -305,7 +316,7 @@
                         q[d, x_at, y_at] = product(stacked(delta), w[dev, d, node])
                 return carry
 
-            lax.fori_loop(0, devices, edges, 0)
+            lax.fori_loop(0, devices, edges, 0, unroll=2 if devices % 2 == 0 else 1)
 
             def gather(y, acc):
                 for i in range(nx):
@@ -382,18 +393,19 @@
     flat_links = links.reshape(len(OFFSETS), nodes).T.astype(jnp.float32)
     flat_links = jnp.pad(flat_links, ((0, 0), (0, B - len(OFFSETS))))
     small = jnp.concatenate([shift.reshape(nodes, B), flat_links], axis=1)
-    small = lax.all_gather(small, GRID_AXES)
     columns = load.reshape(nodes, devices, ROWS, B).transpose(1, 0, 2, 3)
-    columns = lax.all_to_all(columns, GRID_AXES, 0, 0)
-    down, small, columns = lax.optimization_barrier((down, small, columns))
     left = shifted(jnp.stack([masked[1], down[1]]), "gy", 2, 1)
     right = shifted(down[2:], "gy", 2, -1)
     behind = jnp.stack([down[0], left[0], left[1], right[0]])
     inverse = invert(
         masked.reshape(4, nodes, B, B), behind.reshape(4, nodes, B, B), shift.reshape(nodes, B)
     )
-    gathered, inverse = lax.optimization_barrier((gathered, inverse))
+    gathered, inverse, small, columns = lax.optimization_barrier(
+        (gathered, inverse, small, columns)
+    )
     inverses = lax.all_gather(inverse, GRID_AXES)
+    columns = lax.all_to_all(columns, GRID_AXES, 0, 0)
+    small = lax.all_gather(small, GRID_AXES)
     springs = springs_of(gathered, small)
     outs = solve(columns, small, springs, inverses, gx * nbx, gy * nby, nbx, nby)
     outs = lax.all_to_all(outs, GRID_AXES, 0, 0)

time: 167 us -> 156 us (0.934)
  blocking collectives: 31.6 us -> 20.3 us
  Pallas kernels: 79.2 us -> 76.2 us
  waiting for transfers between devices: 20.9 us -> 22.6 us
    all_gather x1, waiting for transfers between devices: 20.2 us -> 2.21 us  [local_columns(): inverses = lax.all_gather(inverse, GRID_AXES)]
    ppermute x2, waiting for transfers between devices: 0.01 us -> 17.1 us  [shifted(): rim = lax.ppermute(rim, axis, [(i, i + 1) for i in range(count - 1)])]
    all_gather x1, blocking collectives: 22.1 us -> 10.7 us  [local_columns(): small = lax.all_gather(small, GRID_AXES)]
    pallas_call x1, Pallas kernels: 39.4 us -> 34.6 us  [solve(): pl.pallas_call(solve_kernel(nx, ny, nbx, nby), out_shape=jax.ShapeDtypeSt...]
    all_to_all x1, starting transfers between devices: 3.37 us -> 6.12 us  [local_columns(): columns = lax.all_to_all(columns, GRID_AXES, 0, 0)]
    ppermute x1, waiting for transfers between devices: 0.01 us -> 2.59 us  [shifted(): rim = lax.ppermute(rim, axis, [(i + 1, i) for i in range(count - 1)])]
    pallas_call x1, Pallas kernels: 28.6 us -> 30.4 us  [invert(): pl.pallas_call(invert_kernel, out_shape=jax.ShapeDtypeStruct((pairs * B +...]
    ppermute x2, starting transfers between devices: 7.97 us -> 6.23 us  [shifted(): rim = lax.ppermute(rim, axis, [(i, i + 1) for i in range(count - 1)])]
  transfers between devices with their start and end apart: 6 -> 6, of which waited for: 1 -> 3; matrix products, arithmetic and copies ran while one was open for 4% -> 4% of each run, Pallas kernels for 24% -> 27%
where the time goes in v4:
time: 156 us; the launch traced here: 155 us
  Pallas kernels  76.2 us (49%)
  waiting for transfers between devices  22.6 us (14%)
  blocking collectives  20.3 us (13%)
  between operations  14.2 us (9%)
  starting transfers between devices  13.7 us (9%)
  other arithmetic  5.25 us (3%)
  local copies, waits for them, and re-layouts  2.88 us (2%)
    pallas_call x1, Pallas kernels, solve(): pl.pallas_call(solve_kernel(nx, ny, nbx, nby), out_shape=jax.ShapeDtypeSt...  34.6 us
    pallas_call x1, Pallas kernels, invert(): pl.pallas_call(invert_kernel, out_shape=jax.ShapeDtypeStruct((pairs * B +...  30.4 us
    ppermute x2, waiting for transfers between devices, shifted(): rim = lax.ppermute(rim, axis, [(i, i + 1) for i in range(count - 1)])  17.1 us
    pallas_call x1, Pallas kernels, springs_of(): pl.pallas_call(spring_kernel, grid=(devices,), out_shape=jax.ShapeDtypeSt...  11.2 us
    all_gather x1, blocking collectives, local_columns(): small = lax.all_gather(small, GRID_AXES)  10.7 us
    all_to_all x1, blocking collectives, local_columns(): outs = lax.all_to_all(outs, GRID_AXES, 0, 0)  9.51 us
    ppermute x2, starting transfers between devices, shifted(): rim = lax.ppermute(rim, axis, [(i, i + 1) for i in range(count - 1)])  6.23 us
    all_to_all x1, starting transfers between devices, local_columns(): columns = lax.all_to_all(columns, GRID_AXES, 0, 0)  6.12 us
  transfers between devices with their start and end apart: 6, of which 3 were waited for; matrix products, arithmetic and copies ran while one was open for 4% of the time, Pallas kernels for 27%

profile of v4, /device:TPU:0, one launch (start us, length us, event | category | flops | bytes accessed | tf_op | source)
XLA Modules:
  0.0 155.1 jit_solution(7944192786773018824)
XLA Ops:
  7.2 0.7 all-gather.7.cloned.1.call-update
  7.9 0.0 all-gather.9.cloned.1.call-start
  8.0 0.8 fusion.7
  8.7 1.2 bitcast_multiply_fusion
  10.1 0.1 pad_maximum_fusion.1
  10.1 4.9 %collective-permute-start = (bf16[3,1,6,128,128]{4,3,2,0,1:T(8,128)(2,1)S(1)}, bf16[3,1,6,128,128]{4,3,2,0,1:T(8,128)(2,1)S(1)}, u32[]{:S(2)}, u32[]{:S(2)}) collective-permute-start(bf16[3,1,6,128,128]{4,3,2,0,1:T(8,128)(2,1)S(1)} %pad_maximum_fusion.1), channel_id=1, source_target_pairs={{0,4},{1,5},{2,6},{3,7},{8,12},{9,13},{10,14},{11,15},{16,20},{17,... | collective-permute-start | bytes 1769480 | tf_op jit(solution)/shard_map/ppermute | solution.py:379
  15.1 0.7 copy.24
  15.7 0.1 copy.14
  15.8 2.2 %fusion.8.ahead = bf16[4,6,128,128]{3,2,1,0:T(8,128)(2,1)} fusion(bf16[4,6]{1,0:T(4,128)(2,1)S(1)} %bitcast.37, bf16[4,1,6,128,128]{4,3,2,1,0:T(8,128)(2,1)} %param.5), kind=kLoop, calls=%fused_computation.17 | loop fusion | flops 393216 | bytes 1572912 | tf_op jit(solution)/shard_map/reshape | solution.py:401
  18.0 17.1 %collective-permute-done = bf16[3,1,6,128,128]{4,3,2,0,1:T(8,128)(2,1)S(1)} collective-permute-done((bf16[3,1,6,128,128]{4,3,2,0,1:T(8,128)(2,1)S(1)}, bf16[3,1,6,128,128]{4,3,2,0,1:T(8,128)(2,1)S(1)}, u32[]{:S(2)}, u32[]{:S(2)}) %collective-permute-start) | collective-permute-done | bytes 589856 | tf_op jit(solution)/shard_map/ppermute | solution.py:379
  35.2 1.3 collective-permute-start.1
  36.5 1.3 collective-permute-start.2
  37.8 0.7 copy.23
  38.5 2.6 %collective-permute-done.2 = bf16[1,1,1,128,128]{4,3,2,0,1:T(8,128)(2,1)S(1)} collective-permute-done((bf16[1,1,1,128,128]{4,3,2,0,1:T(8,128)(2,1)S(1)}, bf16[1,1,1,128,128]{4,3,2,0,1:T(8,128)(2,1)S(1)}, u32[]{:S(2)}, u32[]{:S(2)}) %collective-permute-start.2) | collective-permute-done | bytes 32800 | tf_op jit(solution)/shard_map/ppermute | solution.py:382
  41.1 1.0 fusion.3.behind
  42.1 30.4 %shard_map.59 = f32[392,128]{1,0:T(8,128)} custom-call(bf16[4,6,128,128]{3,2,1,0:T(8,128)(2,1)} %fusion.8.ahead, bf16[4,6,128,128]{3,2,1,0:T(8,128)(2,1)} %fusion.3.behind, f32[6,128]{1,0:T(8,128)} %bitcast.33), custom_call_target="tpu_custom_call" | custom-call | tf_op jit(solution)/shard_map/pallas_call | solution.py:200
  72.5 6.1 %all-to-all-start = ((f32[8,6,4,128]{3,2,1,0:T(4,128)}), f32[8,6,4,128]{3,2,1,0:T(4,128)S(1)}, u32[]{:S(2)}, u32[]{:S(2)}) async-start(f32[8,6,4,128]{3,2,1,0:T(4,128)} %bitcast.23), calls=%async_computation | async-start | bytes 196608 | tf_op jit(solution)/shard_map/all_to_all | solution.py:407
  78.6 10.7 %all-gather.3.small = f32[8,6,256]{2,1,0:T(8,128)} all-gather(f32[1,6,256]{2,1,0:T(8,128)S(1)} %bitcast.34), channel_id=3, replica_groups=mesh['case'=4,'gx'=2,'gy'=4] {'gx','gy'}, dimensions={0}, use_global_device_ids=true | all-gather | bytes 55296 | tf_op jit(solution)/shard_map/all_gather | solution.py:408
  89.4 11.2 %shard_map.60.springs = bf16[8,4,6,128,256]{4,3,2,1,0:T(8,128)(2,1)} custom-call(bf16[8,4,6,128,128]{4,3,2,1,0:T(8,128)(2,1)} %bitcast.26, f32[8,6,256]{2,1,0:T(8,128)} %all-gather.3.small), custom_call_target="tpu_custom_call" | custom-call | tf_op jit(solution)/shard_map/pallas_call | solution.py:221
  100.6 2.2 %all-gather.9.cloned.1.call-done = f32[3136,128]{1,0:T(8,128)} async-done(((f32[392,128]{1,0:T(8,128)}), f32[3136,128]{1,0:T(8,128)}) %all-gather.9.cloned.1.call-update) | async-done | bytes 1605648 | tf_op jit(solution)/shard_map/all_gather | solution.py:406
  102.8 34.6 %shard_map.61 = f32[8,2,6,4,128]{4,3,2,1,0:T(4,128)} custom-call(f32[8,6,4,128]{3,2,1,0:T(4,128)} %copy-done, f32[8,6,256]{2,1,0:T(8,128)} %all-gather.3.small, bf16[8,4,6,128,256]{4,3,2,1,0:T(8,128)(2,1)} %shard_map.60.springs, f32[8,392,128]{2,1,0:T(8,128)} %bitcast.27), custom_call_target="tpu_custom_call" | custom-call | tf_op jit(solution)/shard_map/pallas_call | solution.py:357
  137.4 9.5 %all_to_all.10 = f32[8,2,6,4,128]{4,3,2,1,0:T(4,128)S(1)} all-to-all(f32[8,2,6,4,128]{4,3,2,1,0:T(4,128)} %shard_map.61), channel_id=1, replica_groups=mesh['case'=4,'gx'=2,'gy'=4] {'gx','gy'}, dimensions={0} | all-to-all | bytes 393216 | tf_op jit(solution)/shard_map/all_to_all | solution.py:411
  147.0 0.7 copy.16
  147.6 0.7 copy.17
  (20 shorter events, 0.2 us)
Async XLA Ops:
  7.2 30.6 %copy-start.1 = (f32[1,6,32,128]{3,2,1,0:T(8,128)S(1)}, f32[1,6,32,128]{3,2,1,0:T(8,128)}, u32[]{:S(2)}) copy-start(f32[1,6,32,128]{3,2,1,0:T(8,128)} %param.4) | copy-start | bytes 294916
  7.2 65.3 %all-gather.7.cloned.1.call-start = ((), (), s32[]{:S(2)}) async-start(), calls=%async_computation.2 | async-start | bytes 7077888 | tf_op jit(solution)/shard_map/all_gather | solution.py:390
  7.9 94.9 %all-gather.9.cloned.1.call-start = ((), (), s32[]{:S(2)}) async-start(), calls=%async_computation.3 | async-start | bytes 1806336 | tf_op jit(solution)/shard_map/all_gather | solution.py:406
  10.1 25.0 %collective-permute-start = (bf16[3,1,6,128,128]{4,3,2,0,1:T(8,128)(2,1)S(1)}, bf16[3,1,6,128,128]{4,3,2,0,1:T(8,128)(2,1)S(1)}, u32[]{:S(2)}, u32[]{:S(2)}) collective-permute-start(bf16[3,1,6,128,128]{4,3,2,0,1:T(8,128)(2,1)S(1)} %pad_maximum_fusion.1), channel_id=1, source_target_pairs={{0,4},{1,5},{2,6},{3,7},{8,12},{9,13},{10,14},{11,15},{16,20},{17,... | collective-permute-start | bytes 1769480 | tf_op jit(solution)/shard_map/ppermute | solution.py:379
  15.7 26.3 %copy-start.2 = (f32[1,6,128]{2,1,0:T(8,128)}, f32[1,6,128]{2,1,0:T(8,128)S(1)}, u32[]{:S(2)}) copy-start(f32[1,6,128]{2,1,0:T(8,128)S(1)} %copy.24) | copy-start | bytes 9220
  35.2 5.9 %collective-permute-start.1 = (bf16[2,1,1,128,128]{4,3,2,0,1:T(8,128)(2,1)S(1)}, bf16[2,1,1,128,128]{4,3,2,0,1:T(8,128)(2,1)S(1)}, u32[]{:S(2)}, u32[]{:S(2)}) collective-permute-start(bf16[2,1,1,128,128]{4,3,2,0,1:T(8,128)(2,1)S(1)} %pad_maximum_fusion.2), channel_id=1, source_target_pairs={{0,1},{1,2},{2,3},{4,5},{5,6},{6,7},{8,9},{9,10},{10,11},{12,13},{... | collective-permute-start | bytes 196616 | tf_op jit(solution)/shard_map/ppermute | solution.py:379
  36.5 4.6 %collective-permute-start.2 = (bf16[1,1,1,128,128]{4,3,2,0,1:T(8,128)(2,1)S(1)}, bf16[1,1,1,128,128]{4,3,2,0,1:T(8,128)(2,1)S(1)}, u32[]{:S(2)}, u32[]{:S(2)}) collective-permute-start(bf16[1,1,1,128,128]{4,3,2,0,1:T(8,128)(2,1)S(1)} %slice.60), channel_id=1, source_target_pairs={{1,0},{2,1},{3,2},{5,4},{6,5},{7,6},{9,8},{10,9},{11,10},{13,12},{... | collective-permute-start | bytes 98312 | tf_op jit(solution)/shard_map/ppermute | solution.py:382
  72.5 28.1 %all-to-all-start = ((f32[8,6,4,128]{3,2,1,0:T(4,128)}), f32[8,6,4,128]{3,2,1,0:T(4,128)S(1)}, u32[]{:S(2)}, u32[]{:S(2)}) async-start(f32[8,6,4,128]{3,2,1,0:T(4,128)} %bitcast.23), calls=%async_computation | async-start | bytes 196608 | tf_op jit(solution)/shard_map/all_to_all | solution.py:407
  100.6 2.2 %copy-start = (f32[8,6,4,128]{3,2,1,0:T(4,128)}, f32[8,6,4,128]{3,2,1,0:T(4,128)S(1)}, u32[]{:S(2)}) copy-start(f32[8,6,4,128]{3,2,1,0:T(4,128)S(1)} %all-to-all-done.load) | copy-start | bytes 294916
Sparse Core Ops, SparseCore 0:
  9.9 54.5 all-gather.6
  72.6 30.1 all-gather.8
